TPU v7x, 16 devices: a whole 2x2x2 slice. The times are simulated.
16 devices in a mesh: tp: 4 (over z, y), ep: 4 (over x, core).
Axes of the slice: x: 2, y: 2, z: 2, core: 2. Of those that a mesh axis runs over, the one named last changes fastest.
Arguments:
- x_tok: bfloat16 [32768, 512], P('ep')
- dy_tok: bfloat16 [32768, 512], P('ep')
- route_idx: int32 [32768, 2], P('ep')
- norm_scale: float32 [512], replicated
- w_router: float32 [512, 32], replicated
- w_gate: bfloat16 [32, 512, 2048], P('ep', None, 'tp')
- w_lin: bfloat16 [32, 512, 2048], P('ep', None, 'tp')
- w_out: bfloat16 [32, 2048, 512], P('ep', 'tp')
Outputs:
- output 1: bfloat16 [32768, 512], P('ep')
- output 2: float32 [2], replicated
- output 3: bfloat16 [32768, 512], P('ep')
- output 4: float32 [512], replicated
- output 5: float32 [512, 32], replicated
- output 6: float32 [32, 512, 2048], P('ep', None, 'tp')
- output 7: float32 [32, 512, 2048], P('ep', None, 'tp')
- output 8: float32 [32, 2048, 512], P('ep', 'tp')
All inputs are finite; a program needn't handle non-finite values.
Results may differ from a plain program's by a relative error of at most 0.0165257.
Values are sent between devices in bfloat16 or wider.
A program may use at most 1 GiB of HBM per device.

v0:
```python
import jax
import jax.numpy as jnp
from jax import lax
from jax.sharding import PartitionSpec as P

NORM_EPS = 1e-6
Z_COEF = 0.001
AUX_COEF = 0.01


def gelu_fn(pre_act):
    return jax.nn.gelu(pre_act, approximate=True)


def route_slots(route_ids, experts, slot_cap, stride):
    expert_ids = jnp.arange(experts, dtype=jnp.int32)
    hit_first = (route_ids[:, 0:1] == expert_ids).astype(jnp.int32)
    hit_second = (route_ids[:, 1:2] == expert_ids).astype(jnp.int32)
    rank_first = jnp.cumsum(hit_first, axis=0) - hit_first
    rank_second = jnp.cumsum(hit_second, axis=0) - hit_second + jnp.sum(hit_first, axis=0)
    pos_first = jnp.sum(rank_first * hit_first, axis=1)
    pos_second = jnp.sum(rank_second * hit_second, axis=1)
    overflow = experts * stride
    slot_first = jnp.where(pos_first < slot_cap, route_ids[:, 0] * stride + pos_first, overflow)
    slot_second = jnp.where(pos_second < slot_cap, route_ids[:, 1] * stride + pos_second, overflow)
    return slot_first, slot_second


def slot_tables(slot_first, slot_second, gate_first, gate_second, slot_total):
    tok_count = slot_first.shape[0]
    tok_ids = jnp.arange(tok_count, dtype=jnp.int32)
    slot_tok = jnp.full((slot_total + 1,), tok_count, jnp.int32)
    slot_tok = slot_tok.at[slot_first].set(tok_ids).at[slot_second].set(tok_ids)
    slot_gate = jnp.zeros((slot_total + 1,), jnp.float32)
    slot_gate = slot_gate.at[slot_first].set(gate_first).at[slot_second].set(gate_second)
    return slot_tok[:slot_total], slot_gate[:slot_total]


def pick_rows(row_data, slot_index):
    return jnp.take(row_data, slot_index, axis=0, mode='fill', fill_value=0)


def solution(mesh):
    ep_size = mesh.shape['ep']

    def device_block(x_loc, dy_loc, idx_loc, norm_scale, w_router, gate_loc, lin_loc, out_loc):
        tok_count, model_width = x_loc.shape
        experts = w_router.shape[1]
        local_exp = gate_loc.shape[0]
        tokens = tok_count * ep_size
        slot_cap = (5 * tok_count + 2 * experts - 1) // (2 * experts)
        x_wide = x_loc.astype(jnp.float32)
        inv_rms = lax.rsqrt(jnp.mean(x_wide * x_wide, axis=-1, keepdims=True) + NORM_EPS)
        x_norm = x_wide * inv_rms
        u_tok = (x_norm * norm_scale).astype(jnp.bfloat16)
        u_wide = u_tok.astype(jnp.float32)
        logits = jnp.dot(u_wide, w_router, preferred_element_type=jnp.float32)
        log_norm = jax.nn.logsumexp(logits, axis=-1)
        router_prob = jnp.exp(logits - log_norm[:, None])
        expert_ids = jnp.arange(experts, dtype=jnp.int32)
        one_first = (idx_loc[:, 0:1] == expert_ids).astype(jnp.float32)
        one_second = (idx_loc[:, 1:2] == expert_ids).astype(jnp.float32)
        first_count = lax.psum(jnp.sum(one_first, axis=0), 'ep')
        prob_sum = lax.psum(jnp.sum(router_prob, axis=0), 'ep')
        norm_sq = lax.psum(jnp.sum(log_norm * log_norm), 'ep')
        frac_first = first_count / tokens
        z_loss = Z_COEF * norm_sq / tokens
        aux_loss = AUX_COEF * experts * jnp.sum(frac_first * prob_sum) / tokens
        gate_first = jnp.sum(router_prob * one_first, axis=-1)
        gate_second = jnp.sum(router_prob * one_second, axis=-1)
        gate_total = gate_first + gate_second
        norm_first = gate_first / gate_total
        norm_second = gate_second / gate_total
        slot_first, slot_second = route_slots(idx_loc, experts, slot_cap, slot_cap)
        slot_tok, slot_gate = slot_tables(slot_first, slot_second, norm_first, norm_second, experts * slot_cap)
        disp_rows = pick_rows(u_tok, slot_tok).reshape(experts, slot_cap, model_width)
        recv_rows = lax.all_to_all(disp_rows, 'ep', 0, 0, tiled=True).reshape(ep_size, local_exp, slot_cap, model_width)
        a_gate = jnp.einsum('sxcd,xdf->sxcf', recv_rows, gate_loc, preferred_element_type=jnp.float32)
        a_lin = jnp.einsum('sxcd,xdf->sxcf', recv_rows, lin_loc, preferred_element_type=jnp.float32)
        gelu_val, gelu_back = jax.vjp(gelu_fn, a_gate)
        hidden = (gelu_val * a_lin).astype(jnp.bfloat16)
        part_out = jnp.einsum('sxcf,xfd->sxcd', hidden, out_loc, preferred_element_type=jnp.float32).astype(jnp.bfloat16)
        exp_out = lax.psum(part_out, 'tp')
        back_rows = lax.all_to_all(exp_out.reshape(experts, slot_cap, model_width), 'ep', 0, 0, tiled=True).reshape(experts * slot_cap, model_width)
        out_first = pick_rows(back_rows, slot_first).astype(jnp.float32)
        out_second = pick_rows(back_rows, slot_second).astype(jnp.float32)
        y_loc = (x_wide + norm_first[:, None] * out_first + norm_second[:, None] * out_second).astype(jnp.bfloat16)
        dy_wide = dy_loc.astype(jnp.float32)
        dn_first = jnp.sum(dy_wide * out_first, axis=-1)
        dn_second = jnp.sum(dy_wide * out_second, axis=-1)
        do_slot = (pick_rows(dy_loc, slot_tok).astype(jnp.float32) * slot_gate[:, None]).astype(jnp.bfloat16)
        do_recv = lax.all_to_all(do_slot.reshape(experts, slot_cap, model_width), 'ep', 0, 0, tiled=True).reshape(ep_size, local_exp, slot_cap, model_width)
        d_hidden = jnp.einsum('sxcd,xfd->sxcf', do_recv, out_loc, preferred_element_type=jnp.float32)
        da_gate = gelu_back(d_hidden * a_lin)[0].astype(jnp.bfloat16)
        da_lin = (d_hidden * gelu_val).astype(jnp.bfloat16)
        d_out = jnp.einsum('sxcf,sxcd->xfd', hidden, do_recv, preferred_element_type=jnp.float32)
        d_gate = jnp.einsum('sxcd,sxcf->xdf', recv_rows, da_gate, preferred_element_type=jnp.float32)
        d_lin = jnp.einsum('sxcd,sxcf->xdf', recv_rows, da_lin, preferred_element_type=jnp.float32)
        du_part = jnp.einsum('sxcf,xdf->sxcd', da_gate, gate_loc, preferred_element_type=jnp.float32) + jnp.einsum('sxcf,xdf->sxcd', da_lin, lin_loc, preferred_element_type=jnp.float32)
        du_slot = lax.psum(du_part.astype(jnp.bfloat16), 'tp')
        du_back = lax.all_to_all(du_slot.reshape(experts, slot_cap, model_width), 'ep', 0, 0, tiled=True).reshape(experts * slot_cap, model_width)
        du_exp = pick_rows(du_back, slot_first).astype(jnp.float32) + pick_rows(du_back, slot_second).astype(jnp.float32)
        gate_mix = norm_first * dn_first + norm_second * dn_second
        aux_coef = AUX_COEF * experts * frac_first
        d_logits = router_prob * (aux_coef - jnp.sum(aux_coef * router_prob, axis=-1, keepdims=True))
        d_logits = d_logits + (2.0 * Z_COEF) * log_norm[:, None] * router_prob
        d_logits = d_logits + one_first * (norm_first * (dn_first - gate_mix))[:, None]
        d_logits = d_logits + one_second * (norm_second * (dn_second - gate_mix))[:, None]
        d_router = lax.psum(jnp.einsum('td,te->de', u_wide, d_logits, preferred_element_type=jnp.float32), 'ep')
        du_all = du_exp + jnp.einsum('te,de->td', d_logits, w_router, preferred_element_type=jnp.float32)
        d_scale = lax.psum(jnp.sum(du_all * x_norm, axis=0), 'ep')
        dx_norm = du_all * norm_scale
        dx_loc = (dy_wide + inv_rms * (dx_norm - x_norm * jnp.mean(dx_norm * x_norm, axis=-1, keepdims=True))).astype(jnp.bfloat16)
        losses = jnp.stack([z_loss, aux_loss])
        return (y_loc, losses, dx_loc, d_scale, d_router, d_gate, d_lin, d_out)

    tok_spec = P('ep', None)
    in_spec = P('ep', None, 'tp')
    out_spec = P('ep', 'tp', None)
    return jax.shard_map(device_block, mesh=mesh, in_specs=(tok_spec, tok_spec, tok_spec, P(), P(), in_spec, in_spec, out_spec), out_specs=(tok_spec, P(), tok_spec, P(), P(), in_spec, in_spec, out_spec), check_vma=False)
```

profile of v0, /device:TPU:0, one launch (start us, length us, event | category | flops | bytes accessed | tf_op | source)
XLA Modules:
  0.0 2378.0 jit_solution(13487692118861793510)
XLA Ops:
  7.2 1.0 fusion.75
  8.3 9.5 reduce-window.14
  17.8 0.9 slice_reduce_fusion.1
  19.4 9.5 reduce-window.16
  29.0 0.9 slice_reduce_fusion
  30.4 0.9 convert_reduce_fusion
  32.3 1.1 compare_select_fusion.1
  33.4 30.5 %scatter_custom_fusion = s32[20481]{0:T(1024)S(1)} fusion(s32[8192]{0:T(1024)S(1)} %bitcast.156, s32[8192]{0:T(1024)S(1)} %iota.18, s32[]{:T(128)} %constant.39.clone.1), kind=kCustom, calls=%fused_computation.124 | custom fusion | bytes 81928 | tf_op jit(solution)/shard_map/scatter | solution.py:33
  63.9 30.5 %scatter_fusion = s32[20481]{0:T(1024)S(1)} fusion(s32[20481]{0:T(1024)S(1)} %scatter_custom_fusion, s32[8192]{0:T(1024)S(1)} %bitcast.152, s32[8192]{0:T(1024)S(1)} %iota.19), kind=kCustom, calls=%fused_computation.7 | custom fusion | bytes 131072 | tf_op jit(solution)/shard_map/scatter | solution.py:33
  94.5 5.1 fusion.35
  99.7 7.8 fusion.30
  107.5 87.4 %gather_fusion = bf16[20480,512]{1,0:T(8,128)(2,1)} fusion(bf16[8192,512]{1,0:T(8,128)(2,1)} %fusion.30, s32[20480]{0:T(1024)S(1)} %fusion.65), kind=kCustom, calls=%fused_computation.clone | custom fusion | bytes 42024960 | tf_op jit(solution)/shard_map/jit(_take)/gather | solution.py:40
  194.9 17.9 broadcast_select_fusion
  212.8 7.9 all-to-all-start
  221.0 229.1 %psum.51 = f32[32]{0:T(128)S(1)} all-reduce(f32[32]{0:T(128)S(1)} %convert_reduce_fusion.1), channel_id=1, replica_groups=mesh['tp'=4,'ep'=4] {'ep'}, use_global_device_ids=true, to_apply=%region_18.21 | all-reduce | flops 32 | bytes 256 | tf_op jit(solution)/shard_map/psum | solution.py:63
  450.1 5.9 fusion.76
  457.0 1.3 multiply_reduce_fusion
  458.3 30.5 %scatter_custom_fusion.2 = f32[20481]{0:T(1024)S(1)} fusion(s32[8192]{0:T(1024)S(1)} %bitcast.157, f32[8192]{0:T(1024)S(1)} %get-tuple-element.35, f32[]{:T(128)} %constant.23.clone.1), kind=kCustom, calls=%fused_computation.122 | custom fusion | bytes 81928 | tf_op jit(solution)/shard_map/scatter | solution.py:35
  488.8 30.5 %scatter_fusion.1 = f32[20481]{0:T(1024)S(1)} fusion(f32[20481]{0:T(1024)S(1)} %scatter_custom_fusion.2, s32[8192]{0:T(1024)S(1)} %bitcast.153, f32[8192]{0:T(1024)S(1)} %get-tuple-element.36), kind=kCustom, calls=%fused_computation.9 | custom fusion | bytes 131072 | tf_op jit(solution)/shard_map/scatter | solution.py:35
  519.4 87.4 %gather_fusion.3 = bf16[20480,512]{1,0:T(8,128)(2,1)} fusion(bf16[8192,512]{1,0:T(8,128)(2,1)} %param.13, s32[20480]{0:T(1024)S(1)} %fusion.65), kind=kCustom, calls=%fused_computation.2.clone | custom fusion | bytes 42024960 | tf_op jit(solution)/shard_map/jit(_take)/gather | solution.py:40
  606.8 16.2 multiply_convert_fusion
  623.1 7.8 all-to-all-start.2
  631.1 24.5 %fusion.24 = f32[8,4,640,512]{3,2,1,0:T(8,128)} fusion(bf16[4,8,640,512]{3,2,1,0:T(8,128)(2,1)} %bitcast.11, bf16[8,512,512]{2,1,0:T(8,128)(2,1)} %param.18), kind=kOutput, calls=%fused_computation.53 | convolution fusion | flops 10737418240 | bytes 67108864 | tf_op jit(solution)/shard_map/sxcd,xdf->sxcf/dot_general | solution.py:79
  655.6 24.8 %fusion.26 = f32[8,4,640,512]{3,2,1,0:T(8,128)} fusion(bf16[4,8,640,512]{3,2,1,0:T(8,128)(2,1)} %bitcast.11, bf16[8,512,512]{2,1,0:T(8,128)(2,1)} %param.17), kind=kOutput, calls=%fused_computation.55 | convolution fusion | flops 10737418240 | bytes 67108864 | tf_op jit(solution)/shard_map/sxcd,xdf->sxcf/dot_general | solution.py:78
  680.4 178.0 %all-to-all-done.2 = bf16[32,640,512]{2,1,0:T(8,128)(2,1)} async-done(((bf16[32,640,512]{2,1,0:T(8,128)(2,1)}), bf16[32,640,512]{2,1,0:T(8,128)(2,1)}, u32[]{:S(2)}, u32[]{:S(2)}) %all-to-all-start.2) | async-done | bytes 20971552 | tf_op jit(solution)/shard_map/all_to_all | solution.py:92
  858.5 64.5 %fusion.7 = (bf16[4,8,640,512]{3,2,0,1:T(8,128)(2,1)}, bf16[4,8,640,512]{3,2,0,1:T(8,128)(2,1)}, bf16[4,8,640,512]{3,2,0,1:T(8,128)(2,1)}) fusion(f32[8,4,640,512]{3,2,1,0:T(8,128)} %fusion.26, f32[8,4,640,512]{3,2,1,0:T(8,128)} %fusion.24, bf16[8,512,512]{2,1,0:T(8,128)(2,1)} %param.19, bf16[4,8,640,512]{3,2,1,0:T(8,128)(2,1)} %bitcast.26), kind=kOutput, calls=%fused_computation.21 | convolution fusion | flops 11010048000 | bytes 171966464 | tf_op jit(solution)/shard_map/sxcd,xfd->sxcf/dot_general | solution.py:93
  922.9 24.9 %fusion.41 = f32[8,4,640,512]{3,2,1,0:T(8,128)} fusion(bf16[4,8,640,512]{3,2,0,1:T(8,128)(2,1)} %get-tuple-element.28, bf16[8,512,512]{2,1,0:T(8,128)(2,1)} %param.17), kind=kOutput, calls=%fused_computation.73 | convolution fusion | flops 10737418240 | bytes 67108864 | tf_op jit(solution)/shard_map/sxcf,xdf->sxcd/dot_general | solution.py:99
  947.9 29.9 %fusion.15 = bf16[4,8,640,512]{3,2,0,1:T(8,128)(2,1)} fusion(f32[8,4,640,512]{3,2,1,0:T(8,128)} %fusion.41, bf16[4,8,640,512]{3,2,0,1:T(8,128)(2,1)} %get-tuple-element.27, bf16[8,512,512]{2,1,0:T(8,128)(2,1)} %param.18), kind=kOutput, calls=%fused_computation.42 | convolution fusion | flops 10758389760 | bytes 88080384 | tf_op jit(solution)/shard_map/sxcf,xdf->sxcd/dot_general | solution.py:99
  977.8 17.6 copy.23
  995.4 22.8 convert_bitcast_fusion
  1018.1 17.3 copy.21
  1035.5 708.4 %all-reduce.7.cloned.1.call-done = (bf16[32,640,512]{2,1,0:T(8,128)(2,1)}, bf16[32,640,512]{2,1,0:T(8,128)(2,1)}) async-done(((bf16[32,640,512]{2,1,0:T(8,128)(2,1)}, bf16[32,640,512]{2,1,0:T(8,128)(2,1)}), (bf16[32,640,512]{2,1,0:T(8,128)(2,1)}, bf16[32,640,512]{2,1,0:T(8,128)(2,1)})) %all-reduce.7.cloned.1.call-update) | async-done | bytes 41943056 | tf_op jit(solution)/shard_map/psum | solution.py:83
  1743.9 240.5 %all_to_all.20 = bf16[32,640,512]{2,1,0:T(8,128)(2,1)} all-to-all(bf16[32,640,512]{2,1,0:T(8,128)(2,1)} %get-tuple-element.23), channel_id=1, replica_groups=mesh['tp'=4,'ep'=4] {'ep'}, dimensions={0} | all-to-all | bytes 41943040 | tf_op jit(solution)/shard_map/all_to_all | solution.py:84
  1984.5 7.9 all-to-all-start.3
  1993.7 22.9 fusion.46
  2016.6 22.8 fusion.49
  2039.5 22.9 fusion.52
  2062.4 43.4 %gather_fusion.2 = bf16[8192,512]{1,0:T(8,128)(2,1)} fusion(bf16[20480,512]{1,0:T(8,128)(2,1)} %bitcast.127, s32[8192]{0:T(1024)S(1)} %broadcast_clamp_fusion), kind=kCustom, calls=%fused_computation.3.clone | custom fusion | bytes 16809984 | tf_op jit(solution)/shard_map/jit(_take)/gather | solution.py:40
  2105.8 43.8 %gather_fusion.1 = bf16[8192,512]{1,0:T(8,128)(2,1)} fusion(bf16[20480,512]{1,0:T(8,128)(2,1)} %bitcast.128, s32[8192]{0:T(1024)S(1)} %broadcast_clamp_fusion.1), kind=kCustom, calls=%fused_computation.1.clone | custom fusion | bytes 16809984 | tf_op jit(solution)/shard_map/jit(_take)/gather | solution.py:40
  2149.6 70.4 %all-to-all-done.3 = bf16[32,640,512]{2,1,0:T(8,128)(2,1)} async-done(((bf16[32,640,512]{2,1,0:T(8,128)(2,1)}), bf16[32,640,512]{2,1,0:T(8,128)(2,1)}, u32[]{:S(2)}, u32[]{:S(2)}) %all-to-all-start.3) | async-done | bytes 20971552 | tf_op jit(solution)/shard_map/all_to_all | solution.py:101
  2220.0 43.4 %gather_fusion.5 = bf16[8192,512]{1,0:T(8,128)(2,1)} fusion(bf16[20480,512]{1,0:T(8,128)(2,1)} %bitcast.33, s32[8192]{0:T(1024)S(1)} %broadcast_clamp_fusion), kind=kCustom, calls=%fused_computation.5.clone | custom fusion | bytes 16809984 | tf_op jit(solution)/shard_map/jit(_take)/gather | solution.py:40
  2263.4 43.4 %gather_fusion.4 = bf16[8192,512]{1,0:T(8,128)(2,1)} fusion(bf16[20480,512]{1,0:T(8,128)(2,1)} %bitcast.33, s32[8192]{0:T(1024)S(1)} %broadcast_clamp_fusion.1), kind=kCustom, calls=%fused_computation.4.clone | custom fusion | bytes 16809984 | tf_op jit(solution)/shard_map/jit(_take)/gather | solution.py:40
  2307.0 15.7 fusion.36
  2322.8 5.5 fusion.70
  2328.3 17.5 fusion.34
  2345.8 6.3 all-reduce
  2352.8 14.8 fusion.38
  2369.5 1.5 copy.66
  (101 shorter events, 6.5 us)
Async XLA Ops:
  7.2 442.9 %copy-start = (f32[512,32]{0,1:T(8,128)S(1)}, f32[512,32]{0,1:T(8,128)}, u32[]{:S(2)}) copy-start(f32[512,32]{0,1:T(8,128)} %param.16) | copy-start | bytes 196612
  8.2 448.8 %copy-start.3 = (s32[8192,1]{0,1:T(1,128)}, s32[8192,1]{0,1:T(1,128)S(1)}, u32[]{:S(2)}) copy-start(s32[8192,1]{0,1:T(1,128)S(1)} %get-tuple-element.38) | copy-start | bytes 98308
  8.2 448.8 %copy-start.6 = (s32[8192,1]{0,1:T(1,128)}, s32[8192,1]{0,1:T(1,128)S(1)}, u32[]{:S(2)}) copy-start(s32[8192,1]{0,1:T(1,128)S(1)} %get-tuple-element.37) | copy-start | bytes 98308
  31.4 2.0 copy-start.11
  32.3 62.2 %copy-start.13 = (s32[8192]{0:T(1024)}, s32[8192]{0:T(1024)S(1)}, u32[]{:S(2)}) copy-start(s32[8192]{0:T(1024)S(1)} %fusion.60) | copy-start | bytes 98308
  63.9 35.8 %copy-start.26 = (f32[512]{0:T(512)S(1)}, f32[512]{0:T(512)}, u32[]{:S(2)}) copy-start(f32[512]{0:T(512)} %param.15) | copy-start | bytes 6148
  99.6 95.2 %copy-start.20 = (f32[8192]{0:T(1024)}, f32[8192]{0:T(1024)S(1)}, u32[]{:S(2)}) copy-start(f32[8192]{0:T(1024)S(1)} %add_rsqrt_fusion) | copy-start | bytes 98308
  212.8 410.3 %all-to-all-start = ((bf16[32,640,512]{2,1,0:T(8,128)(2,1)}), bf16[32,640,512]{2,1,0:T(8,128)(2,1)}, u32[]{:S(2)}, u32[]{:S(2)}) async-start(bf16[32,640,512]{2,1,0:T(8,128)(2,1)} %bitcast.129), calls=%async_computation | async-start | bytes 41943040 | tf_op jit(solution)/shard_map/all_to_all | solution.py:77
  450.1 8.2 copy-start.32
  456.0 2.3 copy-start.1
  456.3 63.1 %copy-start.29 = (f32[32]{0:T(128)}, f32[32]{0:T(128)S(1)}, u32[]{:S(2)}) copy-start(f32[32]{0:T(128)S(1)} %broadcast_multiply_fusion.2) | copy-start | bytes 388
  457.0 62.4 %copy-start.17 = (f32[8192]{0:T(1024)}, f32[8192]{0:T(1024)S(1)}, u32[]{:S(2)}) copy-start(f32[8192]{0:T(1024)S(1)} %get-tuple-element.26) | copy-start | bytes 98308
  458.3 30.5 %copy-start.15 = (f32[8192]{0:T(1024)}, f32[8192]{0:T(1024)S(1)}, u32[]{:S(2)}) copy-start(f32[8192]{0:T(1024)S(1)} %get-tuple-element.35) | copy-start | bytes 98308
  458.3 61.1 %copy-start.9 = (f32[8192]{0:T(1024)}, f32[8192]{0:T(1024)S(1)}, u32[]{:S(2)}) copy-start(f32[8192]{0:T(1024)S(1)} %get-tuple-element.36) | copy-start | bytes 98308
  623.1 235.4 %all-to-all-start.2 = ((bf16[32,640,512]{2,1,0:T(8,128)(2,1)}), bf16[32,640,512]{2,1,0:T(8,128)(2,1)}, u32[]{:S(2)}, u32[]{:S(2)}) async-start(bf16[32,640,512]{2,1,0:T(8,128)(2,1)} %bitcast.130), calls=%async_computation.2 | async-start | bytes 41943040 | tf_op jit(solution)/shard_map/all_to_all | solution.py:92
  630.8 1113.1 %all-reduce.7.cloned.1.call-start = ((), (), s32[]{:S(2)}) async-start(), calls=%async_computation.5 | async-start | bytes 83886080 | tf_op jit(solution)/shard_map/psum | solution.py:83
  977.8 17.6 copy-start.31
  1984.4 7.9 copy-start.18
  1984.4 8.6 copy-start.7
  1984.4 8.6 copy-start.14
  1984.4 8.6 copy-start.4
  1984.5 8.6 copy-start.12
  1984.5 235.5 %all-to-all-start.3 = ((bf16[32,640,512]{2,1,0:T(8,128)(2,1)}), bf16[32,640,512]{2,1,0:T(8,128)(2,1)}, u32[]{:S(2)}, u32[]{:S(2)}) async-start(bf16[32,640,512]{2,1,0:T(8,128)(2,1)} %get-tuple-element.24), calls=%async_computation.3 | async-start | bytes 41943040 | tf_op jit(solution)/shard_map/all_to_all | solution.py:101
  1992.3 377.1 %all-reduce.5.cloned.1.call-start = ((), (), s32[]{:S(2)}) async-start(), calls=%async_computation.4 | async-start | bytes 131072 | tf_op jit(solution)/shard_map/psum | solution.py:109
  2263.4 43.4 %copy-start.10 = (f32[8192]{0:T(1024)S(1)}, f32[8192]{0:T(1024)}, u32[]{:S(2)}) copy-start(f32[8192]{0:T(1024)} %copy-done.9) | copy-start | bytes 98308
  2263.4 43.4 %copy-start.16 = (f32[8192]{0:T(1024)S(1)}, f32[8192]{0:T(1024)}, u32[]{:S(2)}) copy-start(f32[8192]{0:T(1024)} %copy-done.15) | copy-start | bytes 98308
  2263.4 43.5 %copy-start.22 = (pred[8192]{0:T(1024)(128)(4,1)S(1)}, pred[8192]{0:T(1024)(128)(4,1)}, u32[]{:S(2)}) copy-start(pred[8192]{0:T(1024)(128)(4,1)} %get-tuple-element.42) | copy-start | bytes 24580
  2263.4 43.5 %copy-start.23 = (pred[8192]{0:T(1024)(128)(4,1)S(1)}, pred[8192]{0:T(1024)(128)(4,1)}, u32[]{:S(2)}) copy-start(pred[8192]{0:T(1024)(128)(4,1)} %get-tuple-element.43) | copy-start | bytes 24580
  2306.9 15.8 copy-start.2
  2306.9 15.8 copy-start.5
  2306.9 15.8 copy-start.8
  2306.9 15.8 copy-start.19
  2306.9 15.8 copy-start.24
  2307.0 15.8 copy-start.25
  2307.0 15.8 copy-start.30
  2307.0 21.3 copy-start.21
  2307.0 21.3 copy-start.27
  2328.3 17.5 copy-start.28
  2328.3 23.8 %copy-start.33 = (f32[32]{0:T(128)S(1)}, f32[32]{0:T(128)}, u32[]{:S(2)}) copy-start(f32[32]{0:T(128)} %copy-done.32) | copy-start | bytes 388
Sparse Core Ops, SparseCore 0:
  1035.6 708.2 all-reduce.6
  2328.4 29.0 all-reduce.4
where the time goes:
time: 2390 us; the launch traced here: 2380 us
  waiting for transfers between devices  957 us (40%)
  local copies, waits for them, and re-layouts  510 us (21%)
  blocking collectives  476 us (20%)
  matrix products  289 us (12%)
  other arithmetic  106 us (4%)
    psum x1, waiting for transfers between devices, device_block(): exp_out = lax.psum(part_out, 'tp')  708 us
    gather x6, local copies, waits for them, and re-layouts, pick_rows(): return jnp.take(row_data, slot_index, axis=0, mode='fill', fill_value=0)  349 us
    all_to_all x1, blocking collectives, device_block(): lax.all_to_all(exp_out.reshape(experts, slot_cap, model_width), 'ep', 0,...  241 us
    psum x1, blocking collectives, device_block(): first_count = lax.psum(jnp.sum(one_first, axis=0), 'ep')  229 us
    all_to_all x1, waiting for transfers between devices, device_block(): lax.all_to_all(do_slot.reshape(experts, slot_cap, model_width), 'ep', 0,...  178 us
    all_to_all x1, waiting for transfers between devices, device_block(): lax.all_to_all(du_slot.reshape(experts, slot_cap, model_width), 'ep', 0,...  70.4 us
    dot_general x1, matrix products, device_block(): jnp.einsum('sxcd,xfd->sxcf', do_recv, out_loc, preferred_element_type=jnp...  64.5 us
    scatter x2, local copies, waits for them, and re-layouts, slot_tables(): slot_gate.at[slot_first].set(gate_first).at[slot_second].set(gate_second)  61 us
  transfers between devices with their start and end apart: 5, of which 3 were waited for; matrix products, arithmetic and copies ran while one was open for 17% of the time, Pallas kernels for 0%

commit v1 on v0

v1 whole, which is shorter than its diff:
```python
import functools

import jax
import jax.numpy as jnp
from jax import lax
from jax.experimental import pallas as pl
from jax.experimental.pallas import tpu as pltpu
from jax.sharding import PartitionSpec as P


NORM_EPS = 1e-6
Z_COEF = 0.001
AUX_COEF = 0.01
GELU_C = 0.7978845608028654
GELU_K = 0.044715
BF = jnp.bfloat16
F32 = jnp.float32
TILE = 320
CHUNKS = 2
NT = (((1,), (1,)), ((), ()))
TN = (((0,), (0,)), ((), ()))


def widen_kernel(start_ref, x_ref, dy_ref, out_ref, wide):
    count = x_ref.shape[0]
    for j in range(4):
        lanes = slice(128 * j, 128 * (j + 1))
        wide[pl.ds(j, count, stride=8), :] = x_ref[:, lanes].astype(F32)
        wide[pl.ds(4 + j, count, stride=8), :] = dy_ref[:, lanes].astype(F32)
    out_ref[...] = wide[...].reshape(count, 8, 128).astype(BF)


def widen_rows(x, dy, start, count):
    block = 512
    width = x.shape[1]
    source = pl.BlockSpec((block, width), lambda i, first: (first[0] + i, 0))
    first = jnp.full((1,), start // block, jnp.int32)
    return pl.pallas_call(
        widen_kernel,
        grid_spec=pltpu.PrefetchScalarGridSpec(
            num_scalar_prefetch=1,
            grid=(count // block,),
            in_specs=[source, source],
            out_specs=pl.BlockSpec((block, 8, 128), lambda i, _: (i, 0, 0)),
            scratch_shapes=[pltpu.VMEM((block * 8, 128), F32)],
        ),
        out_shape=jax.ShapeDtypeStruct((count, 8, 128), BF),
        compiler_params=pltpu.CompilerParams(dimension_semantics=("arbitrary",), vmem_limit_bytes=60 * 1024 * 1024),
        cost_estimate=pl.CostEstimate(flops=count * 1_000_000, bytes_accessed=count * width * 8, transcendentals=0),
        name="widen_rows",
    )(first, x, dy)


def expert_kernel(n_piece, has_acc, has_prev, cap, idx_ref, *refs):
    pieces = refs[:n_piece]
    refs = refs[n_piece:]
    gate_ref, scale_ref, wg_ref, wl_ref, wo_ref = refs[:5]
    refs = refs[5:]
    acc_refs = refs[:3] if has_acc else None
    refs = refs[3:] if has_acc else refs
    refs = refs[2:] if has_prev else refs
    o_ref, du_ref, dg_ref, dl_ref, do_ref, table, rows, sems = refs
    step = pl.program_id(0)
    piece_rows = table.shape[0] // n_piece

    @pl.when(step == 0)
    def _():
        copies = [
            pltpu.make_async_copy(pieces[i], table.at[pl.ds(i * piece_rows, piece_rows)], sems.at[i])
            for i in range(n_piece)
        ]
        for c in copies:
            c.start()
        for c in copies:
            c.wait()

    base = step * cap

    def pick(i, _):
        for k in range(16):
            r = i * 16 + k
            rows[pl.ds(pl.multiple_of(r * 8, 8), 8), :] = table[idx_ref[base + r]].astype(F32)
        return 0

    lax.fori_loop(0, cap // 16, pick, 0)

    for out, i in ((dg_ref, 0), (dl_ref, 1), (do_ref, 2)):
        out[...] = acc_refs[i][...] if has_acc else jnp.zeros_like(out)

    wg, wl, wo = wg_ref[0], wl_ref[0], wo_ref[0]

    def tile(t, _):
        r0 = pl.multiple_of(t * TILE, TILE)

        def cols(j):
            return rows[pl.ds(r0 * 8 + j, TILE, stride=8), :]

        x = jnp.concatenate([cols(j) for j in range(4)], axis=1)
        gv = gate_ref[0, pl.ds(r0, TILE), :]
        inv = lax.rsqrt(jnp.mean(x * x, axis=-1, keepdims=True) + NORM_EPS)
        inv = jnp.where(gv[:, 1:2] > 0.0, inv, 0.0)
        u = (x * inv * scale_ref[...]).astype(BF)
        a0 = jnp.dot(u, wg, preferred_element_type=F32)
        a1 = jnp.dot(u, wl, preferred_element_type=F32)
        sq = a0 * a0
        th = jnp.tanh(GELU_C * a0 * (1.0 + GELU_K * sq))
        half = 0.5 * (1.0 + th)
        ge = a0 * half
        gp = half + 0.5 * a0 * (1.0 - th * th) * (GELU_C * (1.0 + 3.0 * GELU_K * sq))
        h = (ge * a1).astype(BF)
        o = jnp.dot(h, wo, preferred_element_type=F32).astype(BF)
        for k in range(4):
            o_ref[k, pl.ds(r0, TILE), :] = o[:, 128 * k:128 * (k + 1)]
        dy = jnp.concatenate([cols(4 + j) for j in range(4)], axis=1)
        d_o = (dy * gv[:, 0:1]).astype(BF)
        dh = lax.dot_general(d_o, wo, NT, preferred_element_type=F32)
        da0 = (dh * a1 * gp).astype(BF)
        da1 = (dh * ge).astype(BF)
        du = lax.dot_general(da0, wg, NT, preferred_element_type=F32)
        du = (du + lax.dot_general(da1, wl, NT, preferred_element_type=F32)).astype(BF)
        for k in range(4):
            du_ref[k, pl.ds(r0, TILE), :] = du[:, 128 * k:128 * (k + 1)]
        dg_ref[0] += lax.dot_general(u, da0, TN, preferred_element_type=F32)
        dl_ref[0] += lax.dot_general(u, da1, TN, preferred_element_type=F32)
        do_ref[0] += lax.dot_general(h, d_o, TN, preferred_element_type=F32)
        return 0

    lax.fori_loop(0, cap // TILE, tile, 0)


def run_experts(idx, pieces, gates, scale, wg, wl, wo, acc, prev):
    experts, cap, _ = gates.shape
    width, ff = wg.shape[1:]
    tokens = sum(p.shape[0] for p in pieces)
    n_piece = len(pieces)
    has_acc = acc is not None
    any_spec = pl.BlockSpec(memory_space=pl.ANY)
    by_exp = lambda *s: pl.BlockSpec((1,) + s, lambda e, _: (e, 0, 0))
    in_specs = [any_spec] * n_piece + [
        by_exp(cap, 2),
        pl.BlockSpec((1, width), lambda e, _: (0, 0)),
        by_exp(width, ff), by_exp(width, ff), by_exp(ff, width),
    ]
    args = list(pieces) + [gates, scale, wg, wl, wo]
    grad_specs = [by_exp(width, ff), by_exp(width, ff), by_exp(ff, width)]
    grad_shapes = [jax.ShapeDtypeStruct(w.shape, F32) for w in (wg, wl, wo)]
    aliases = {}
    if has_acc:
        for i in range(3):
            aliases[1 + len(args) + i] = 2 + i
        in_specs += grad_specs
        args += list(acc)
    lanes = width // 4
    shift = 0
    if prev is not None:
        for i in range(2):
            aliases[1 + len(args) + i] = i
        in_specs += [any_spec] * 2
        args += list(prev)
        shift = experts
    row_spec = pl.BlockSpec((4, cap, lanes), lambda e, _: (0, e + shift, 0))
    row_shape = jax.ShapeDtypeStruct((4, 2 * experts * cap, lanes), BF)
    flops = 2 * 9 * experts * cap * width * ff
    moved = tokens * width * 4 + experts * cap * width * 4 + 3 * width * ff * experts * (2 + 4 + 4 * has_acc)
    return pl.pallas_call(
        functools.partial(expert_kernel, n_piece, has_acc, prev is not None, cap),
        grid_spec=pltpu.PrefetchScalarGridSpec(
            num_scalar_prefetch=1,
            grid=(experts,),
            in_specs=in_specs,
            out_specs=[row_spec, row_spec] + grad_specs,
            scratch_shapes=[
                pltpu.VMEM((tokens, 8, 128), BF),
                pltpu.VMEM((cap * 8, 128), F32),
                pltpu.SemaphoreType.DMA((n_piece,)),
            ],
        ),
        out_shape=[row_shape, row_shape] + grad_shapes,
        input_output_aliases=aliases,
        compiler_params=pltpu.CompilerParams(
            dimension_semantics=("arbitrary",), vmem_limit_bytes=60 * 1024 * 1024),
        cost_estimate=pl.CostEstimate(flops=flops, bytes_accessed=moved, transcendentals=experts * cap * ff),
        name="experts_acc" if has_acc else "experts_new",
    )(idx, *args)


def collect_kernel(idx_ref, *refs):
    parts, refs = refs[:4], refs[4:]
    first_ref, second_ref, raw, table, sems = refs
    part_rows = parts[0].shape[0]
    copies = [
        pltpu.make_async_copy(parts[i], raw.at[pl.ds(i * part_rows, part_rows)], sems.at[i])
        for i in range(4)
    ]
    for c in copies:
        c.start()
    table[pl.ds(4 * part_rows, 8), :] = jnp.zeros((8, table.shape[1]), F32)
    for i in range(4):
        copies[i].wait()

        def widen(b, _):
            r = pl.multiple_of(i * part_rows + b * 128, 128)
            table[pl.ds(r, 128), :] = raw[pl.ds(r, 128), :].astype(F32)
            return 0

        lax.fori_loop(0, part_rows // 128, widen, 0)

    def pick(b, _):
        for k in range(8):
            t = b * 8 + k
            first_ref[pl.ds(t, 1), :] = table[pl.ds(idx_ref[0, t], 1), :]
            second_ref[pl.ds(t, 1), :] = table[pl.ds(idx_ref[1, t], 1), :]
        return 0

    lax.fori_loop(0, first_ref.shape[0] // 8, pick, 0)


def collect_rows(idx, parts):
    count = idx.shape[1]
    part_rows, lanes = parts[0].shape
    whole = pl.BlockSpec((count, lanes), lambda i, _: (0, 0))
    shape = jax.ShapeDtypeStruct((count, lanes), F32)
    return pl.pallas_call(
        collect_kernel,
        grid_spec=pltpu.PrefetchScalarGridSpec(
            num_scalar_prefetch=1,
            grid=(1,),
            in_specs=[pl.BlockSpec(memory_space=pl.ANY)] * 4,
            out_specs=[whole, whole],
            scratch_shapes=[
                pltpu.VMEM((4 * part_rows, lanes), BF),
                pltpu.VMEM((4 * part_rows + 8, lanes), F32),
                pltpu.SemaphoreType.DMA((4,)),
            ],
        ),
        out_shape=[shape, shape],
        compiler_params=pltpu.CompilerParams(
            dimension_semantics=("arbitrary",), vmem_limit_bytes=48 * 1024 * 1024),
        cost_estimate=pl.CostEstimate(flops=20_000_000_000, bytes_accessed=14_000_000, transcendentals=0),
        name="collect_rows",
    )(idx, *parts)


def choice_positions(idx_loc, experts):
    tok_count = idx_loc.shape[0]
    block = 128
    ids = jnp.arange(experts, dtype=jnp.int32)
    hit1 = idx_loc[:, 0:1] == ids
    hit2 = idx_loc[:, 1:2] == ids
    hits = jnp.concatenate([hit1, hit2], axis=1).astype(BF)
    blocks = hits.reshape(tok_count // block, block, 2 * experts)
    tri = (jnp.arange(block)[:, None] > jnp.arange(block)[None, :]).astype(BF)
    inner = jnp.einsum('ij,bjk->bik', tri, blocks, preferred_element_type=F32)
    sums = jnp.sum(blocks.astype(F32), axis=1)
    outer = jnp.cumsum(sums, axis=0) - sums
    count = jnp.sum(sums, axis=0)
    outer = outer + jnp.concatenate([jnp.zeros_like(count[:experts]), count[:experts]])
    rank = (inner + outer[:, None, :]).reshape(tok_count, 2 * experts)
    rank = rank * hits.astype(F32)
    pos1 = jnp.sum(rank[:, :experts], axis=1).astype(jnp.int32)
    pos2 = jnp.sum(rank[:, experts:], axis=1).astype(jnp.int32)
    return hit1, hit2, pos1, pos2, count[:experts]


def split3(v):
    hi = v.astype(BF)
    rest = v - hi.astype(F32)
    mid = rest.astype(BF)
    return hi, mid, (rest - mid.astype(F32)).astype(BF)


def slot_table(hit1, hit2, pos1, pos2, g1, g2, cap):
    tok_count, experts = hit1.shape
    tok = jnp.arange(1, tok_count + 1, dtype=jnp.int32)
    hi = (tok // 128).astype(BF)
    lo = (tok % 128).astype(BF)
    slots = jnp.arange(cap, dtype=jnp.int32)
    total = 0.0
    for hit, pos, g in ((hit1, pos1, g1), (hit2, pos2, g2)):
        vals = (hi, lo) + split3(g)
        left = jnp.concatenate([jnp.where(hit, v[:, None], BF(0)) for v in vals], axis=1)
        at = (pos[:, None] == slots).astype(BF)
        total = total + jnp.einsum('tk,tc->kc', left, at, preferred_element_type=F32)
    total = total.reshape(5, experts, cap)
    tok1 = total[0] * 128.0 + total[1]
    gate = (total[2] + total[3]) + total[4]
    return tok1, gate


def solution(mesh):
    ep_size = mesh.shape['ep']
    tp_size = mesh.shape['tp']

    def swap(v, bit):
        return lax.ppermute(v, 'ep', [(i, i ^ bit) for i in range(ep_size)])

    def device_block(x_loc, dy_loc, idx_loc, norm_scale, w_router, gate_loc, lin_loc, out_loc):
        tok_count, width = x_loc.shape
        experts = w_router.shape[1]
        local_exp = gate_loc.shape[0]
        tokens = tok_count * ep_size
        slot_cap = (5 * tok_count + 2 * experts - 1) // (2 * experts)
        ep_idx = lax.axis_index('ep')
        tp_idx = lax.axis_index('tp')
        quarter = tok_count // tp_size
        lanes = width // tp_size

        q_start = tp_idx * quarter
        part = quarter // CHUNKS
        sent, cuts = [], []
        for c in range(CHUNKS):
            rows = widen_rows(x_loc, dy_loc, q_start + c * part, part)
            cuts.append(rows)
            sent.append(swap(rows, 2))
        x_own, dy_own, _ = lax.optimization_barrier((x_loc, dy_loc, cuts))
        own = widen_rows(x_own, dy_own, 0, tok_count)
        partner = swap(own, 1)
        far = []
        for c in range(CHUNKS):
            far.append(lax.all_gather(sent[c], 'tp', tiled=True))
        far_partner = [swap(f, 1) for f in far]

        x_wide = x_loc.astype(F32)
        inv_rms = lax.rsqrt(jnp.mean(x_wide * x_wide, axis=-1, keepdims=True) + NORM_EPS)
        x_norm = x_wide * inv_rms
        u_tok = (x_norm * norm_scale).astype(BF)
        u_wide = u_tok.astype(F32)
        logits = jnp.dot(u_wide, w_router, preferred_element_type=F32)
        log_norm = jax.nn.logsumexp(logits, axis=-1)
        router_prob = jnp.exp(logits - log_norm[:, None])
        hit1, hit2, pos1, pos2, count_loc = choice_positions(idx_loc, experts)
        one_first = hit1.astype(F32)
        one_second = hit2.astype(F32)
        stats = jnp.concatenate([count_loc, jnp.sum(router_prob, axis=0), jnp.sum(log_norm * log_norm)[None]])
        gate_first = jnp.sum(router_prob * one_first, axis=-1)
        gate_second = jnp.sum(router_prob * one_second, axis=-1)
        gate_total = gate_first + gate_second
        norm_first = gate_first / gate_total
        norm_second = gate_second / gate_total

        tok1, slot_gate = slot_table(hit1, hit2, pos1, pos2, norm_first, norm_second, slot_cap)
        info = jnp.stack([tok1, slot_gate], axis=1)
        info = lax.all_to_all(info, 'ep', 0, 0, tiled=True).reshape(ep_size, local_exp, 2, slot_cap)

        scale_row = norm_scale[None, :]
        acc = None
        pairs = []
        for rel, pieces in enumerate(([own], [partner], far, far_partner)):
            mine = lax.dynamic_index_in_dim(info, ep_idx ^ rel, 0, keepdims=False)
            tok = mine[:, 0].astype(jnp.int32)
            valid = (tok > 0).astype(F32)
            tok = jnp.maximum(tok - 1, 0)
            if len(pieces) > 1:
                q, rest = tok // quarter, tok % quarter
                tok = (rest // part) * (tp_size * part) + q * part + rest % part
            gates = jnp.stack([mine[:, 1], valid], axis=-1)
            prev = (o, du) if rel % 2 else None
            o, du, *acc = run_experts(tok.reshape(-1), pieces, gates, scale_row, gate_loc, lin_loc, out_loc, acc, prev)
            if rel % 2:
                pairs.append((o, du))
        d_gate, d_lin, d_out = acc
        (o_near, du_near), (o_far, du_far) = pairs
        stats, o_far = lax.optimization_barrier((stats, o_far))
        stats = lax.psum(stats, 'ep')
        frac_first = stats[:experts] / tokens
        z_loss = Z_COEF * stats[2 * experts] / tokens
        aux_loss = AUX_COEF * experts * jnp.sum(frac_first * stats[experts:2 * experts]) / tokens

        def scatter_sum(v):
            flat = v.reshape(-1, v.shape[2])
            return lax.optimization_barrier(lax.psum_scatter(flat, 'tp', scatter_dimension=0, tiled=True))

        def spread(near, far):
            half = near.shape[0] // 2
            return [near[:half], swap(near[half:], 1), swap(far[:half], 2), swap(far[half:], 3)]

        o_near = scatter_sum(o_near)
        o_far = scatter_sum(o_far)
        du_far = scatter_sum(du_far)
        du_near = scatter_sum(du_near)

        def place(ids, pos):
            rel = (ids // local_exp) ^ ep_idx
            slot = (rel * local_exp + ids % local_exp) * slot_cap + pos
            return jnp.where(pos < slot_cap, slot, experts * slot_cap)

        both = jnp.stack([place(idx_loc[:, 0], pos1), place(idx_loc[:, 1], pos2)])

        def fetch(parts):
            return collect_rows(both, parts)

        c_start = tp_idx * lanes
        col = lambda v: lax.dynamic_slice_in_dim(v, c_start, lanes, axis=v.ndim - 1)
        x_col = col(x_loc).astype(F32)
        dy_col = col(dy_loc).astype(F32)
        xn_col = x_col * inv_rms
        scale_col = col(norm_scale)
        u_col = (xn_col * scale_col).astype(BF).astype(F32)
        wr_col = lax.dynamic_slice_in_dim(w_router, c_start, lanes, axis=0)

        o1, o2 = fetch(spread(o_near, o_far))
        y_col = (x_col + norm_first[:, None] * o1 + norm_second[:, None] * o2).astype(BF)
        dn1 = jnp.sum(dy_col * o1, axis=-1)
        dn2 = jnp.sum(dy_col * o2, axis=-1)
        dn_first = lax.psum(dn1, 'tp')
        dn2, dn_first = lax.optimization_barrier((dn2, dn_first))
        dn_second = lax.psum(dn2, 'tp')
        gate_mix = norm_first * dn_first + norm_second * dn_second
        y_col, du_near = lax.optimization_barrier((y_col, du_near))
        aux_coef = AUX_COEF * experts * frac_first
        d_logits = router_prob * (aux_coef - jnp.sum(aux_coef * router_prob, axis=-1, keepdims=True))
        d_logits = d_logits + (2.0 * Z_COEF) * log_norm[:, None] * router_prob
        d_logits = d_logits + one_first * (norm_first * (dn_first - gate_mix))[:, None]
        d_logits = d_logits + one_second * (norm_second * (dn_second - gate_mix))[:, None]
        d_router_col = jnp.einsum('td,te->de', u_col, d_logits, preferred_element_type=F32)
        du_dense = jnp.einsum('te,de->td', d_logits, wr_col, preferred_element_type=F32)

        du1, du2 = fetch(spread(du_near, du_far))
        du_all = du1 + du2 + du_dense
        d_scale_col = jnp.sum(du_all * xn_col, axis=0)
        dxn = du_all * scale_col
        proj = lax.psum(jnp.sum(dxn * xn_col, axis=-1), 'tp')[:, None] / width
        dx_col = (dy_col + inv_rms * (dxn - xn_col * proj)).astype(BF)

        def full(v):
            return lax.all_gather(v, 'tp', axis=1, tiled=True)

        y_loc = full(y_col)
        dx_loc = full(dx_col)
        d_router = lax.all_gather(lax.psum(d_router_col, 'ep'), 'tp', axis=0, tiled=True)
        d_scale = lax.all_gather(lax.psum(d_scale_col, 'ep'), 'tp', axis=0, tiled=True)
        losses = jnp.stack([z_loss, aux_loss])
        return (y_loc, losses, dx_loc, d_scale, d_router, d_gate, d_lin, d_out)

    tok_spec = P('ep', None)
    in_spec = P('ep', None, 'tp')
    out_spec = P('ep', 'tp', None)
    return jax.shard_map(device_block, mesh=mesh, in_specs=(tok_spec, tok_spec, tok_spec, P(), P(), in_spec, in_spec, out_spec), out_specs=(tok_spec, P(), tok_spec, P(), P(), in_spec, in_spec, out_spec), check_vma=False)
```

time: 2390 us -> 989 us (0.41)
  waiting for transfers between devices: 957 us -> 349 us
  local copies, waits for them, and re-layouts: 510 us -> 43.1 us
  Pallas kernels: 0 us -> 355 us
  blocking collectives: 476 us -> 130 us
  matrix products: 289 us -> 22.9 us
  other arithmetic: 106 us -> 42.8 us
    psum x2 -> x0, waiting for transfers between devices: 708 us -> none  [the longest x1 708 us: device_block(): exp_out = lax.psum(part_out, 'tp')]
    pallas_call x0 -> x9, Pallas kernels: none -> 355 us  [the longest x4 256 us: run_experts(): pl.pallas_call(functools.partial(expert_kernel, n_piece, has_acc, prev is...]
    gather x6 -> x0, local copies, waits for them, and re-layouts: 349 us -> none  [pick_rows(): return jnp.take(row_data, slot_index, axis=0, mode='fill', fill_value=0)]
    dot_general x12 -> x6, matrix products: 289 us -> 22.9 us  [the longest x2 10.1 us: slot_table(): jnp.einsum('tk,tc->kc', left, at, preferred_element_type=F32)]
    reduce_scatter x0 -> x4, waiting for transfers between devices: none -> 253 us  [scatter_sum(): lax.psum_scatter(flat, 'tp', scatter_dimension=0, tiled=True)]
    all_to_all x3 -> x1, waiting for transfers between devices: 248 us -> 0.01 us  [device_block(): lax.all_to_all(info, 'ep', 0, 0, tiled=True)]
    all_to_all x1 -> x0, blocking collectives: 241 us -> none  [device_block(): lax.all_to_all(exp_out.reshape(experts, slot_cap, model_width), 'ep', 0,...]
    scatter x4 -> x0, local copies, waits for them, and re-layouts: 122 us -> none  [the longest x2 61 us: slot_tables(): slot_gate.at[slot_first].set(gate_first).at[slot_second].set(gate_second)]
  transfers between devices with their start and end apart: 5 -> 20, of which waited for: 3 -> 6; matrix products, arithmetic and copies ran while one was open for 17% -> 9% of each run, Pallas kernels for 0% -> 36%
where the time goes in v1:
time: 989 us; the launch traced here: 983 us
  Pallas kernels  355 us (36%)
  waiting for transfers between devices  349 us (35%)
  blocking collectives  130 us (13%)
  local copies, waits for them, and re-layouts  43.1 us (4%)
  other arithmetic  42.8 us (4%)
  starting transfers between devices  23.1 us (2%)
  matrix products  22.9 us (2%)
  between operations  16.4 us (2%)
    pallas_call x4, Pallas kernels, run_experts(): pl.pallas_call(functools.partial(expert_kernel, n_piece, has_acc, prev is...  256 us
    reduce_scatter x4, waiting for transfers between devices, scatter_sum(): lax.psum_scatter(flat, 'tp', scatter_dimension=0, tiled=True)  253 us
    pallas_call x2, Pallas kernels, collect_rows(): pl.pallas_call(collect_kernel, grid_spec=pltpu.PrefetchScalarGridSpec(num...  71.9 us
    psum x1, blocking collectives, device_block(): stats = lax.psum(stats, 'ep')  55.1 us
    all_gather x2, waiting for transfers between devices, full(): return lax.all_gather(v, 'tp', axis=1, tiled=True)  49.4 us
    ppermute x11, waiting for transfers between devices, swap(): return lax.ppermute(v, 'ep', [(i, i ^ bit) for i in range(ep_size)])  45.8 us
    pallas_call x3, Pallas kernels, widen_rows(): pl.pallas_call(widen_kernel, grid_spec=pltpu.PrefetchScalarGridSpec(num_s...  27.3 us
  transfers between devices with their start and end apart: 20, of which 6 were waited for; matrix products, arithmetic and copies ran while one was open for 9% of the time, Pallas kernels for 36%

profile of v1, /device:TPU:0, one launch (start us, length us, event | category | flops | bytes accessed | tf_op | source)
XLA Modules:
  0.0 982.5 jit_solution(7036708142858764273)
XLA Ops:
  7.2 3.6 widen_rows.3
  10.9 3.2 collective-permute-start.2
  14.1 3.6 widen_rows.4
  17.7 20.1 %widen_rows.5.refs_0_ = bf16[8192,8,128]{2,1,0:T(8,128)(2,1)} custom-call(s32[1]{0:T(128)} %constant.221.clone.1.start_ref, bf16[8192,512]{1,0:T(8,128)(2,1)} %x_ref.4, bf16[8192,512]{1,0:T(8,128)(2,1)} %dy_ref.4), custom_call_target="tpu_custom_call" | custom-call | flops 8192000000 | bytes 33554432 | tf_op jit(solution)/shard_map/widen_rows/pallas_call | solution.py:38
  39.2 5.1 fusion.2
  44.4 6.4 fusion.101
  50.9 10.0 %collective-permute-done.2 = bf16[1024,8,128]{2,1,0:T(8,128)(2,1)} collective-permute-done((bf16[1024,8,128]{2,1,0:T(8,128)(2,1)}, bf16[1024,8,128]{2,1,0:T(8,128)(2,1)}, u32[]{:S(2)}, u32[]{:S(2)}) %collective-permute-start.2) | collective-permute-done | bytes 2097184 | tf_op jit(solution)/shard_map/ppermute | solution.py:295
  67.0 1.3 copy-done.15
  69.2 35.8 %collective-permute-done.4 = bf16[1024,8,128]{2,1,0:T(8,128)(2,1)} collective-permute-done((bf16[1024,8,128]{2,1,0:T(8,128)(2,1)}, bf16[1024,8,128]{2,1,0:T(8,128)(2,1)}, u32[]{:S(2)}, u32[]{:S(2)}) %collective-permute-start.4) | collective-permute-done | bytes 2097184 | tf_op jit(solution)/shard_map/ppermute | solution.py:295
  105.9 6.0 fusion
  112.1 4.1 fusion.29
  117.0 3.3 all-to-all-start
  120.4 11.5 %reduce-scatter.5.cloned.1.call-start = ((), (), s32[]{:S(2)}) async-start(), calls=%async_computation.5 | async-start | bytes 13107200 | tf_op jit(solution)/shard_map/reduce_scatter | solution.py:371
  132.6 2.3 copy.127.refs_1_
  135.6 2.3 copy.126.refs_1_
  137.8 62.5 %experts_new.1 = (bf16[4,10240,128]{2,1,0:T(8,128)(2,1)}, bf16[4,10240,128]{2,1,0:T(8,128)(2,1)}, f32[8,512,512]{2,1,0:T(8,128)}, f32[8,512,512]{2,1,0:T(8,128)}, f32[8,512,512]{2,1,0:T(8,128)}) custom-call(s32[5120]{0:T(1024)} %max.29.idx_ref, bf16[8192,8,128]{2,1,0:T(8,128)(2,1)} %widen_rows.5.refs_0_, f32[8,640,2]{2,1,0:T(8,128)} %copy.126.refs_1_, ...), custom_call_target="tpu_custom_call" | custom-call | flops 24159191040 | bytes 65011712 | tf_op jit(solution)/shard_map/experts_new/pallas_call | solution.py:165
  200.3 64.2 %experts_acc.3 = (bf16[4,10240,128]{2,1,0:T(8,128)(2,1)}, bf16[4,10240,128]{2,1,0:T(8,128)(2,1)}, f32[8,512,512]{2,1,0:T(8,128)}, f32[8,512,512]{2,1,0:T(8,128)}, f32[8,512,512]{2,1,0:T(8,128)}) custom-call(s32[5120]{0:T(1024)} %max.27.idx_ref, ...), custom_call_target="tpu_custom_call", output_to_operand_aliasing={{2}: (7, {}), {3}: (8, {}), {4}: (9, {}), {0}: (10, {}), {1... | custom-call | flops 24159191040 | bytes 90177536 | tf_op jit(solution)/shard_map/experts_acc/pallas_call | solution.py:165
  266.6 2.3 copy.131.refs_2_
  269.0 2.5 copy.130.refs_2_
  272.7 64.8 %experts_acc.4 = (bf16[4,10240,128]{2,1,0:T(8,128)(2,1)}, bf16[4,10240,128]{2,1,0:T(8,128)(2,1)}, f32[8,512,512]{2,1,0:T(8,128)}, f32[8,512,512]{2,1,0:T(8,128)}, f32[8,512,512]{2,1,0:T(8,128)}) custom-call(s32[5120]{0:T(1024)} %fusion.74.idx_ref, ...), custom_call_target="tpu_custom_call", output_to_operand_aliasing={{2}: (8, {}), {3}: (9, {}), {4}: (10, {})} | custom-call | flops 24159191040 | bytes 90177536 | tf_op jit(solution)/shard_map/experts_acc/pallas_call | solution.py:165
  337.5 64.8 %experts_acc.5 = (bf16[4,10240,128]{2,1,0:T(8,128)(2,1)}, bf16[4,10240,128]{2,1,0:T(8,128)(2,1)}, f32[8,512,512]{2,1,0:T(8,128)}, f32[8,512,512]{2,1,0:T(8,128)}, f32[8,512,512]{2,1,0:T(8,128)}) custom-call(s32[5120]{0:T(1024)} %fusion.70.idx_ref, ...), custom_call_target="tpu_custom_call", output_to_operand_aliasing={{2}: (8, {}), {3}: (9, {}), {4}: (10, {}), {0}: (11, {}), {... | custom-call | flops 24159191040 | bytes 90177536 | tf_op jit(solution)/shard_map/experts_acc/pallas_call | solution.py:165
  403.5 2.9 fusion.99
  406.5 97.5 %reduce-scatter.7.cloned.1.call-done = bf16[10240,128]{1,0:T(8,128)(2,1)} async-done(((bf16[40960,128]{1,0:T(8,128)(2,1)}), bf16[10240,128]{1,0:T(8,128)(2,1)}) %reduce-scatter.7.cloned.1.call-update) | async-done | bytes 2621456 | tf_op jit(solution)/shard_map/reduce_scatter | solution.py:371
  504.0 3.4 fusion.98
  507.5 1.5 collective-permute-start.6
  509.6 97.2 %reduce-scatter.9.cloned.1.call-done = bf16[10240,128]{1,0:T(8,128)(2,1)} async-done(((bf16[40960,128]{1,0:T(8,128)(2,1)}), bf16[10240,128]{1,0:T(8,128)(2,1)}) %reduce-scatter.9.cloned.1.call-update) | async-done | bytes 2621456 | tf_op jit(solution)/shard_map/reduce_scatter | solution.py:371
  606.8 35.8 %collect_rows.2 = (f32[8192,128]{1,0:T(8,128)}, f32[8192,128]{1,0:T(8,128)}) custom-call(s32[2,8192]{1,0:T(2,128)S(1)} %pad_add_fusion.1.idx_ref, bf16[5120,128]{1,0:T(8,128)(2,1)S(1)} %get-tuple-element.100.refs_0_, bf16[5120,128]{1,0:T(8,128)(2,1)S(1)} %collective-permute-done.1.refs_1_, bf16[5120,128]{1,0:T(8,128)(2,1)} %collective-permute-done.6.refs_2_, ...), custom_call_target="tpu_custom_call" | custom-call | flops 20000000000 | bytes 14000000 | tf_op jit(solution)/shard_map/collect_rows/pallas_call | solution.py:223
  642.6 8.5 fusion.23
  651.3 58.2 %reduce-scatter.11.cloned.1.call-done = bf16[10240,128]{1,0:T(8,128)(2,1)} async-done(((bf16[40960,128]{1,0:T(8,128)(2,1)}), bf16[10240,128]{1,0:T(8,128)(2,1)}) %reduce-scatter.11.cloned.1.call-update) | async-done | bytes 2621456 | tf_op jit(solution)/shard_map/reduce_scatter | solution.py:371
  709.4 3.5 fusion.96
  712.9 1.5 collective-permute-start.9
  714.4 3.2 fusion.97
  719.2 55.1 %psum.42 = f32[65]{0:T(128)S(1)} all-reduce(f32[65]{0:T(128)S(1)} %pad_maximum_fusion.5), channel_id=1, replica_groups=mesh['tp'=4,'ep'=4] {'ep'}, use_global_device_ids=true, to_apply=%region_15.16 | all-reduce | flops 65 | bytes 520 | tf_op jit(solution)/shard_map/psum | solution.py:364
  774.9 1.5 multiply_reduce_fusion
  776.4 17.0 %psum.43 = f32[8192]{0:T(1024)S(1)} all-reduce(f32[8192]{0:T(1024)S(1)} %get-tuple-element.74), channel_id=1, replica_groups=mesh['tp'=4,'ep'=4] {'tp'}, use_global_device_ids=true, to_apply=%region_21.22 | all-reduce | flops 8192 | bytes 65536 | tf_op jit(solution)/shard_map/psum | solution.py:405
  793.4 14.7 %psum.44 = f32[8192]{0:T(1024)S(1)} all-reduce(f32[8192]{0:T(1024)S(1)} %get-tuple-element.68), channel_id=1, replica_groups=mesh['tp'=4,'ep'=4] {'tp'}, use_global_device_ids=true, to_apply=%region_22.23 | all-reduce | flops 8192 | bytes 65536 | tf_op jit(solution)/shard_map/psum | solution.py:407
  808.2 2.1 fusion.84
  810.3 36.0 %collect_rows.3 = (f32[8192,128]{1,0:T(8,128)}, f32[8192,128]{1,0:T(8,128)}) custom-call(s32[2,8192]{1,0:T(2,128)S(1)} %pad_add_fusion.1.idx_ref, bf16[5120,128]{1,0:T(8,128)(2,1)S(1)} %get-tuple-element.96.refs_0_, bf16[5120,128]{1,0:T(8,128)(2,1)} %collective-permute-done.8.refs_1_, bf16[5120,128]{1,0:T(8,128)(2,1)S(1)} %collective-permute-done.9.refs_2_, ...), custom_call_target="tpu_custom_call" | custom-call | flops 20000000000 | bytes 14000000 | tf_op jit(solution)/shard_map/collect_rows/pallas_call | solution.py:223
  846.4 6.6 fusion.18
  853.0 15.6 %psum.45 = f32[8192]{0:T(1024)S(1)} all-reduce(f32[8192]{0:T(1024)S(1)} %get-tuple-element.73), channel_id=1, replica_groups=mesh['tp'=4,'ep'=4] {'tp'}, use_global_device_ids=true, to_apply=%region_24.25 | all-reduce | flops 8192 | bytes 65536 | tf_op jit(solution)/shard_map/psum | solution.py:422
  868.6 8.2 fusion.24
  879.3 3.8 fusion.25
  883.1 11.1 %all-reduce.1 = (f32[128]{0:T(128)S(1)}, f32[128,32]{0,1:T(8,128)S(1)}) all-reduce(f32[128]{0:T(128)S(1)} %get-tuple-element.72, f32[128,32]{0,1:T(8,128)S(1)} %fusion.25), channel_id=1, replica_groups=mesh['tp'=4,'ep'=4] {'ep'}, use_global_device_ids=true, to_apply=%region_26.27 | all-reduce | flops 4224 | bytes 33792 | tf_op jit(solution)/shard_map/psum | solution.py:431
  894.1 7.3 all-gather
  901.4 8.8 all_gather.23
  910.2 49.4 %all-gather.12.cloned.1.call-done = bf16[8192,512]{1,0:T(8,128)(2,1)} async-done(((bf16[8192,128]{1,0:T(8,128)(2,1)}), bf16[8192,512]{1,0:T(8,128)(2,1)}) %all-gather.12.cloned.1.call-update) | async-done | bytes 8388624 | tf_op jit(solution)/shard_map/all_gather | solution.py:426
  959.6 7.3 copy.177
  966.9 7.3 copy.178
  (147 shorter events, 21.7 us)
Async XLA Ops:
  7.2 37.2 %copy-start = (f32[512,32]{0,1:T(8,128)S(1)}, f32[512,32]{0,1:T(8,128)}, u32[]{:S(2)}) copy-start(f32[512,32]{0,1:T(8,128)} %param.12) | copy-start | bytes 196612
  7.2 257.4 %all-gather.6.cloned.1.call-start = ((), (), s32[]{:S(2)}) async-start(), calls=%async_computation.6 | async-start | bytes 10485760 | tf_op jit(solution)/shard_map/all_gather | solution.py:320
  10.9 50.0 %collective-permute-start.2 = (bf16[1024,8,128]{2,1,0:T(8,128)(2,1)}, bf16[1024,8,128]{2,1,0:T(8,128)(2,1)}, u32[]{:S(2)}, u32[]{:S(2)}) collective-permute-start(bf16[1024,8,128]{2,1,0:T(8,128)(2,1)} %widen_rows.3), channel_id=1, source_target_pairs={{0,2},{1,3},{2,0},{3,1},{4,6},{5,7},{6,4},{7,5},{8,10},{9,11},{10,... | collective-permute-start | bytes 6291464 | tf_op jit(solution)/shard_map/ppermute | solution.py:295
  17.6 20.2 %copy-start.13 = (s32[8192,2]{0,1:T(2,128)S(1)}, s32[8192,2]{0,1:T(2,128)}, u32[]{:S(2)}) copy-start(s32[8192,2]{0,1:T(2,128)} %param.10) | copy-start | bytes 196612
  17.6 87.3 %collective-permute-start.4 = (bf16[1024,8,128]{2,1,0:T(8,128)(2,1)}, bf16[1024,8,128]{2,1,0:T(8,128)(2,1)}, u32[]{:S(2)}, u32[]{:S(2)}) collective-permute-start(bf16[1024,8,128]{2,1,0:T(8,128)(2,1)} %widen_rows.4), channel_id=1, source_target_pairs={{0,2},{1,3},{2,0},{3,1},{4,6},{5,7},{6,4},{7,5},{8,10},{9,11},{10,... | collective-permute-start | bytes 6291464 | tf_op jit(solution)/shard_map/ppermute | solution.py:295
  37.8 162.5 %collective-permute-start = (bf16[8192,8,128]{2,1,0:T(8,128)(2,1)}, bf16[8192,8,128]{2,1,0:T(8,128)(2,1)}, u32[]{:S(2)}, u32[]{:S(2)}) collective-permute-start(bf16[8192,8,128]{2,1,0:T(8,128)(2,1)} %widen_rows.5.refs_0_), channel_id=1, source_target_pairs={{0,1},{1,0},{2,3},{3,2},{4,5},{5,4},{6,7},{7,6},{8,9},{9,8},{10,11... | collective-permute-start | bytes 50331656 | tf_op jit(solution)/shard_map/ppermute | solution.py:295
  37.9 67.1 %copy-start.3 = (s32[8192,1]{0,1:T(1,128)}, s32[8192,1]{0,1:T(1,128)S(1)}, u32[]{:S(2)}) copy-start(s32[8192,1]{0,1:T(1,128)S(1)} %get-tuple-element.113) | copy-start | bytes 98308
  37.9 74.1 %copy-start.5 = (s32[8192,1]{0,1:T(1,128)}, s32[8192,1]{0,1:T(1,128)S(1)}, u32[]{:S(2)}) copy-start(s32[8192,1]{0,1:T(1,128)S(1)} %get-tuple-element.114) | copy-start | bytes 98308
  39.2 5.2 copy-start.17
  44.4 6.4 copy-start.11
  50.8 13.7 %copy-start.1 = (f32[8192,32]{0,1:T(8,128)}, f32[8192,32]{0,1:T(8,128)S(1)}, u32[]{:S(2)}) copy-start(f32[8192,32]{0,1:T(8,128)S(1)} %get-tuple-element.134) | copy-start | bytes 3145732
  60.9 203.9 %all-gather.8.cloned.1.call-start = ((), (), s32[]{:S(2)}) async-start(), calls=%async_computation.7 | async-start | bytes 10485760 | tf_op jit(solution)/shard_map/all_gather | solution.py:320
  63.3 3.5 copy-start.7
  63.3 3.5 copy-start.9
  66.8 1.5 copy-start.15
  105.9 6.0 copy-start.16
  117.0 14.9 %all-to-all-start = ((f32[32,2,640]{2,1,0:T(2,128)}), f32[32,2,640]{2,1,0:T(2,128)S(1)}, u32[]{:S(2)}, u32[]{:S(2)}) async-start(f32[32,2,640]{2,1,0:T(2,128)} %copy.123), calls=%async_computation | async-start | bytes 327680 | tf_op jit(solution)/shard_map/all_to_all | solution.py:343
  120.4 283.2 %reduce-scatter.5.cloned.1.call-start = ((), (), s32[]{:S(2)}) async-start(), calls=%async_computation.5 | async-start | bytes 13107200 | tf_op jit(solution)/shard_map/reduce_scatter | solution.py:371
  264.5 239.5 %reduce-scatter.7.cloned.1.call-start = ((), (), s32[]{:S(2)}) async-start(), calls=%async_computation.8 | async-start | bytes 13107200 | tf_op jit(solution)/shard_map/reduce_scatter | solution.py:371
  264.6 72.9 %collective-permute-start.3 = (bf16[4096,8,128]{2,1,0:T(8,128)(2,1)}, bf16[4096,8,128]{2,1,0:T(8,128)(2,1)}, u32[]{:S(2)}, u32[]{:S(2)}) collective-permute-start(bf16[4096,8,128]{2,1,0:T(8,128)(2,1)} %all-gather.6.cloned.1.call-done.refs_0_), channel_id=1, source_target_pairs={{0,1},{1,0},{2,3},{3,2},{4,5},{5,4},{6,7},{7,6},{8,9},{9,8},{10,11... | collective-permute-start | bytes 25165832 | tf_op jit(solution)/shard_map/ppermute | solution.py:295
  264.8 72.7 %collective-permute-start.5 = (bf16[4096,8,128]{2,1,0:T(8,128)(2,1)}, bf16[4096,8,128]{2,1,0:T(8,128)(2,1)}, u32[]{:S(2)}, u32[]{:S(2)}) collective-permute-start(bf16[4096,8,128]{2,1,0:T(8,128)(2,1)} %all-gather.8.cloned.1.call-done.refs_1_), channel_id=1, source_target_pairs={{0,1},{1,0},{2,3},{3,2},{4,5},{5,4},{6,7},{7,6},{8,9},{9,8},{10,11... | collective-permute-start | bytes 25165832 | tf_op jit(solution)/shard_map/ppermute | solution.py:295
  402.3 204.4 %reduce-scatter.9.cloned.1.call-start = ((), (), s32[]{:S(2)}) async-start(), calls=%async_computation.9 | async-start | bytes 13107200 | tf_op jit(solution)/shard_map/reduce_scatter | solution.py:371
  402.9 306.5 %reduce-scatter.11.cloned.1.call-start = ((), (), s32[]{:S(2)}) async-start(), calls=%async_computation.11 | async-start | bytes 13107200 | tf_op jit(solution)/shard_map/reduce_scatter | solution.py:371
  403.5 506.8 %all-gather.10.cloned.1.call-start = ((), (), s32[]{:S(2)}) async-start(), calls=%async_computation.10 | async-start | bytes 10485760 | tf_op jit(solution)/shard_map/all_gather | solution.py:426
  406.5 200.3 %collective-permute-start.1 = (bf16[5120,128]{1,0:T(8,128)(2,1)}, bf16[5120,128]{1,0:T(8,128)(2,1)S(1)}, u32[]{:S(2)}, u32[]{:S(2)}) collective-permute-start(bf16[5120,128]{1,0:T(8,128)(2,1)} %get-tuple-element.99), channel_id=1, source_target_pairs={{0,1},{1,0},{2,3},{3,2},{4,5},{5,4},{6,7},{7,6},{8,9},{9,8},{10,11... | collective-permute-start | bytes 3932168 | tf_op jit(solution)/shard_map/ppermute | solution.py:295
  507.5 99.3 %collective-permute-start.6 = (bf16[5120,128]{1,0:T(8,128)(2,1)}, bf16[5120,128]{1,0:T(8,128)(2,1)}, u32[]{:S(2)}, u32[]{:S(2)}) collective-permute-start(bf16[5120,128]{1,0:T(8,128)(2,1)} %get-tuple-element.98), channel_id=1, source_target_pairs={{0,2},{1,3},{2,0},{3,1},{4,6},{5,7},{6,4},{7,5},{8,10},{9,11},{10,... | collective-permute-start | bytes 3932168 | tf_op jit(solution)/shard_map/ppermute | solution.py:295
  508.9 97.8 %collective-permute-start.7 = (bf16[5120,128]{1,0:T(8,128)(2,1)}, bf16[5120,128]{1,0:T(8,128)(2,1)}, u32[]{:S(2)}, u32[]{:S(2)}) collective-permute-start(bf16[5120,128]{1,0:T(8,128)(2,1)} %get-tuple-element.97), channel_id=1, source_target_pairs={{0,3},{1,2},{2,1},{3,0},{4,7},{5,6},{6,5},{7,4},{8,11},{9,10},{10,... | collective-permute-start | bytes 3932168 | tf_op jit(solution)/shard_map/ppermute | solution.py:295
  606.7 35.9 %copy-start.8 = (f32[8192]{0:T(1024)S(1)}, f32[8192]{0:T(1024)}, u32[]{:S(2)}) copy-start(f32[8192]{0:T(1024)} %copy-done.7) | copy-start | bytes 98308
  606.8 35.9 %copy-start.10 = (f32[8192]{0:T(1024)S(1)}, f32[8192]{0:T(1024)}, u32[]{:S(2)}) copy-start(f32[8192]{0:T(1024)} %copy-done.9) | copy-start | bytes 98308
  651.2 308.4 %all-gather.12.cloned.1.call-start = ((), (), s32[]{:S(2)}) async-start(), calls=%async_computation.12 | async-start | bytes 10485760 | tf_op jit(solution)/shard_map/all_gather | solution.py:426
  712.9 95.3 %copy-start.4 = (s32[8192,1]{0,1:T(1,128)S(1)}, s32[8192,1]{0,1:T(1,128)}, u32[]{:S(2)}) copy-start(s32[8192,1]{0,1:T(1,128)} %copy-done.3) | copy-start | bytes 98308
  712.9 95.3 %copy-start.6 = (s32[8192,1]{0,1:T(1,128)S(1)}, s32[8192,1]{0,1:T(1,128)}, u32[]{:S(2)}) copy-start(s32[8192,1]{0,1:T(1,128)} %copy-done.5) | copy-start | bytes 98308
  712.9 95.3 %copy-start.14 = (f32[8192]{0:T(1024)S(1)}, f32[8192]{0:T(1024)}, u32[]{:S(2)}) copy-start(f32[8192]{0:T(1024)} %get-tuple-element.86) | copy-start | bytes 98308
  712.9 97.4 %collective-permute-start.9 = (bf16[5120,128]{1,0:T(8,128)(2,1)}, bf16[5120,128]{1,0:T(8,128)(2,1)S(1)}, u32[]{:S(2)}, u32[]{:S(2)}) collective-permute-start(bf16[5120,128]{1,0:T(8,128)(2,1)} %get-tuple-element.94), channel_id=1, source_target_pairs={{0,2},{1,3},{2,0},{3,1},{4,6},{5,7},{6,4},{7,5},{8,10},{9,11},{10,... | collective-permute-start | bytes 3932168 | tf_op jit(solution)/shard_map/ppermute | solution.py:295
  714.4 95.9 %collective-permute-start.10 = (bf16[5120,128]{1,0:T(8,128)(2,1)}, bf16[5120,128]{1,0:T(8,128)(2,1)}, u32[]{:S(2)}, u32[]{:S(2)}) collective-permute-start(bf16[5120,128]{1,0:T(8,128)(2,1)} %get-tuple-element.93), channel_id=1, source_target_pairs={{0,3},{1,2},{2,1},{3,0},{4,7},{5,6},{6,5},{7,4},{8,11},{9,10},{10,... | collective-permute-start | bytes 3932168 | tf_op jit(solution)/shard_map/ppermute | solution.py:295
  717.6 92.7 %collective-permute-start.8 = (bf16[5120,128]{1,0:T(8,128)(2,1)}, bf16[5120,128]{1,0:T(8,128)(2,1)}, u32[]{:S(2)}, u32[]{:S(2)}) collective-permute-start(bf16[5120,128]{1,0:T(8,128)(2,1)} %get-tuple-element.95), channel_id=1, source_target_pairs={{0,1},{1,0},{2,3},{3,2},{4,5},{5,4},{6,7},{7,6},{8,9},{9,8},{10,11... | collective-permute-start | bytes 3932168 | tf_op jit(solution)/shard_map/ppermute | solution.py:295
  810.3 36.1 %copy-start.12 = (f32[8192]{0:T(1024)S(1)}, f32[8192]{0:T(1024)}, u32[]{:S(2)}) copy-start(f32[8192]{0:T(1024)} %copy-done.11) | copy-start | bytes 98308
  868.6 10.7 %copy-start.2 = (f32[8192,32]{0,1:T(8,128)S(1)}, f32[8192,32]{0,1:T(8,128)}, u32[]{:S(2)}) copy-start(f32[8192,32]{0,1:T(8,128)} %copy-done.1) | copy-start | bytes 3145732
Sparse Core Ops, SparseCore 0:
  61.0 85.3 all-gather.5
  148.2 83.7 all-gather.7
  264.6 101.3 reduce-scatter.4
  402.4 101.5 reduce-scatter.6
  507.0 99.7 reduce-scatter.8
  609.7 99.7 reduce-scatter.10
  711.2 84.9 all-gather.9
  876.9 82.6 all-gather.11

commit v2 on v1

--- a/solution.py
+++ b/solution.py
@@ -15,8 +15,8 @@
 GELU_K = 0.044715
 BF = jnp.bfloat16
 F32 = jnp.float32
-TILE = 320
-CHUNKS = 2
+TILE = 640
+CHUNKS = (3, 5)
 NT = (((1,), (1,)), ((), ()))
 TN = (((0,), (0,)), ((), ()))
 
@@ -31,7 +31,7 @@
 
 
 def widen_rows(x, dy, start, count):
-    block = 512
+    block = 256
     width = x.shape[1]
     source = pl.BlockSpec((block, width), lambda i, first: (first[0] + i, 0))
     first = jnp.full((1,), start // block, jnp.int32)
@@ -59,14 +59,17 @@
     acc_refs = refs[:3] if has_acc else None
     refs = refs[3:] if has_acc else refs
     refs = refs[2:] if has_prev else refs
-    o_ref, du_ref, dg_ref, dl_ref, do_ref, table, rows, sems = refs
+    o_ref, du_ref, dg_ref, dl_ref, do_ref, table, rows, u_all, h_all, dy_all, a0_all, a1_all, sems = refs
     step = pl.program_id(0)
-    piece_rows = table.shape[0] // n_piece
+    starts = [sum(p.shape[0] for p in pieces[:i]) for i in range(n_piece)]
+
+    def pick(base, r):
+        rows[pl.ds(pl.multiple_of(r * 8, 8), 8), :] = table[idx_ref[base + r]].astype(F32)
 
     @pl.when(step == 0)
     def _():
         copies = [
-            pltpu.make_async_copy(pieces[i], table.at[pl.ds(i * piece_rows, piece_rows)], sems.at[i])
+            pltpu.make_async_copy(pieces[i], table.at[pl.ds(starts[i], pieces[i].shape[0])], sems.at[i])
             for i in range(n_piece)
         ]
         for c in copies:
@@ -74,58 +77,62 @@
         for c in copies:
             c.wait()
 
-    base = step * cap
-
-    def pick(i, _):
-        for k in range(16):
-            r = i * 16 + k
-            rows[pl.ds(pl.multiple_of(r * 8, 8), 8), :] = table[idx_ref[base + r]].astype(F32)
-        return 0
-
-    lax.fori_loop(0, cap // 16, pick, 0)
-
-    for out, i in ((dg_ref, 0), (dl_ref, 1), (do_ref, 2)):
-        out[...] = acc_refs[i][...] if has_acc else jnp.zeros_like(out)
-
+        def some(i, _):
+            for k in range(16):
+                pick(0, i * 16 + k)
+            return 0
+
+        lax.fori_loop(0, cap // 16, some, 0)
+
+    later = jnp.minimum(step + 1, pl.num_programs(0) - 1) * cap
     wg, wl, wo = wg_ref[0], wl_ref[0], wo_ref[0]
 
     def tile(t, _):
         r0 = pl.multiple_of(t * TILE, TILE)
+        here = pl.ds(r0, TILE)
 
         def cols(j):
             return rows[pl.ds(r0 * 8 + j, TILE, stride=8), :]
 
         x = jnp.concatenate([cols(j) for j in range(4)], axis=1)
-        gv = gate_ref[0, pl.ds(r0, TILE), :]
+        dy = jnp.concatenate([cols(4 + j) for j in range(4)], axis=1)
+        gv = gate_ref[0, here, :]
         inv = lax.rsqrt(jnp.mean(x * x, axis=-1, keepdims=True) + NORM_EPS)
         inv = jnp.where(gv[:, 1:2] > 0.0, inv, 0.0)
         u = (x * inv * scale_ref[...]).astype(BF)
+        d_o = (dy * gv[:, 0:1]).astype(BF)
+        u_all[here, :] = u
+        dy_all[here, :] = d_o
+        for k in range(TILE):
+            pick(later, r0 + k)
         a0 = jnp.dot(u, wg, preferred_element_type=F32)
         a1 = jnp.dot(u, wl, preferred_element_type=F32)
+        dh = lax.dot_general(d_o, wo, NT, preferred_element_type=F32)
         sq = a0 * a0
         th = jnp.tanh(GELU_C * a0 * (1.0 + GELU_K * sq))
         half = 0.5 * (1.0 + th)
         ge = a0 * half
         gp = half + 0.5 * a0 * (1.0 - th * th) * (GELU_C * (1.0 + 3.0 * GELU_K * sq))
         h = (ge * a1).astype(BF)
+        h_all[here, :] = h
+        da0 = (dh * a1 * gp).astype(BF)
+        da1 = (dh * ge).astype(BF)
+        a0_all[here, :] = da0
+        a1_all[here, :] = da1
         o = jnp.dot(h, wo, preferred_element_type=F32).astype(BF)
         for k in range(4):
-            o_ref[k, pl.ds(r0, TILE), :] = o[:, 128 * k:128 * (k + 1)]
-        dy = jnp.concatenate([cols(4 + j) for j in range(4)], axis=1)
-        d_o = (dy * gv[:, 0:1]).astype(BF)
-        dh = lax.dot_general(d_o, wo, NT, preferred_element_type=F32)
-        da0 = (dh * a1 * gp).astype(BF)
-        da1 = (dh * ge).astype(BF)
+            o_ref[k, here, :] = o[:, 128 * k:128 * (k + 1)]
         du = lax.dot_general(da0, wg, NT, preferred_element_type=F32)
         du = (du + lax.dot_general(da1, wl, NT, preferred_element_type=F32)).astype(BF)
         for k in range(4):
-            du_ref[k, pl.ds(r0, TILE), :] = du[:, 128 * k:128 * (k + 1)]
-        dg_ref[0] += lax.dot_general(u, da0, TN, preferred_element_type=F32)
-        dl_ref[0] += lax.dot_general(u, da1, TN, preferred_element_type=F32)
-        do_ref[0] += lax.dot_general(h, d_o, TN, preferred_element_type=F32)
+            du_ref[k, here, :] = du[:, 128 * k:128 * (k + 1)]
         return 0
 
     lax.fori_loop(0, cap // TILE, tile, 0)
+
+    for i, (out, left, right) in enumerate(((dg_ref, u_all, a0_all), (dl_ref, u_all, a1_all), (do_ref, h_all, dy_all))):
+        grad = lax.dot_general(left[...], right[...], TN, preferred_element_type=F32)
+        out[0] = acc_refs[i][0] + grad if has_acc else grad
 
 
 def run_experts(idx, pieces, gates, scale, wg, wl, wo, acc, prev):
@@ -172,6 +179,11 @@
             scratch_shapes=[
                 pltpu.VMEM((tokens, 8, 128), BF),
                 pltpu.VMEM((cap * 8, 128), F32),
+                pltpu.VMEM((cap, width), BF),
+                pltpu.VMEM((cap, ff), BF),
+                pltpu.VMEM((cap, width), BF),
+                pltpu.VMEM((cap, ff), BF),
+                pltpu.VMEM((cap, ff), BF),
                 pltpu.SemaphoreType.DMA((n_piece,)),
             ],
         ),
@@ -306,17 +318,17 @@
         lanes = width // tp_size
 
         q_start = tp_idx * quarter
-        part = quarter // CHUNKS
+        parts = [quarter * c // sum(CHUNKS) for c in CHUNKS]
         sent, cuts = [], []
-        for c in range(CHUNKS):
-            rows = widen_rows(x_loc, dy_loc, q_start + c * part, part)
+        for c, part in enumerate(parts):
+            rows = widen_rows(x_loc, dy_loc, q_start + sum(parts[:c]), part)
             cuts.append(rows)
             sent.append(swap(rows, 2))
         x_own, dy_own, _ = lax.optimization_barrier((x_loc, dy_loc, cuts))
         own = widen_rows(x_own, dy_own, 0, tok_count)
         partner = swap(own, 1)
         far = []
-        for c in range(CHUNKS):
+        for c in range(len(parts)):
             far.append(lax.all_gather(sent[c], 'tp', tiled=True))
         far_partner = [swap(f, 1) for f in far]
 
@@ -352,7 +364,9 @@
             tok = jnp.maximum(tok - 1, 0)
             if len(pieces) > 1:
                 q, rest = tok // quarter, tok % quarter
-                tok = (rest // part) * (tp_size * part) + q * part + rest % part
+                tok = jnp.where(
+                    rest < parts[0], q * parts[0] + rest,
+                    tp_size * parts[0] + q * parts[1] + rest - parts[0])
             gates = jnp.stack([mine[:, 1], valid], axis=-1)
             prev = (o, du) if rel % 2 else None
             o, du, *acc = run_experts(tok.reshape(-1), pieces, gates, scale_row, gate_loc, lin_loc, out_loc, acc, prev)
@@ -423,10 +437,13 @@
         dx_col = (dy_col + inv_rms * (dxn - xn_col * proj)).astype(BF)
 
         def full(v):
-            return lax.all_gather(v, 'tp', axis=1, tiled=True)
-
-        y_loc = full(y_col)
-        dx_loc = full(dx_col)
+            return lax.all_gather(v, 'tp')
+
+        def join(v):
+            return v.transpose(1, 0, 2).reshape(tok_count, width)
+
+        y_loc = join(full(y_col))
+        dx_loc = join(full(dx_col))
         d_router = lax.all_gather(lax.psum(d_router_col, 'ep'), 'tp', axis=0, tiled=True)
         d_scale = lax.all_gather(lax.psum(d_scale_col, 'ep'), 'tp', axis=0, tiled=True)
         losses = jnp.stack([z_loss, aux_loss])

time: 989 us -> 964 us (0.975)
  Pallas kernels: 355 us -> 312 us
  waiting for transfers between devices: 349 us -> 379 us
  starting transfers between devices: 23.1 us -> 11.7 us
    pallas_call x4, Pallas kernels: 256 us -> 205 us  [run_experts(): pl.pallas_call(functools.partial(expert_kernel, n_piece, has_acc, prev is...]
    all_gather x2, waiting for transfers between devices: 0.02 us -> 24.6 us  [device_block(): far.append(lax.all_gather(sent[c], 'tp', tiled=True))]
    reshape x0 -> x2, local copies, waits for them, and re-layouts: none -> 17.4 us  [join(): return v.transpose(1, 0, 2).reshape(tok_count, width)]
    unnamed x44 -> x36, local copies, waits for them, and re-layouts: 17.2 us -> 2.89 us
    reduce_scatter x4, starting transfers between devices: 11.7 us -> 0.57 us  [scatter_sum(): lax.psum_scatter(flat, 'tp', scatter_dimension=0, tiled=True)]
    ppermute x11, waiting for transfers between devices: 45.8 us -> 56.8 us  [swap(): return lax.ppermute(v, 'ep', [(i, i ^ bit) for i in range(ep_size)])]
  transfers between devices with their start and end apart: 20 -> 20, of which waited for: 6 -> 7; matrix products, arithmetic and copies ran while one was open for 9% -> 10% of each run, Pallas kernels for 36% -> 32%
where the time goes in v2:
time: 964 us; the launch traced here: 959 us
  waiting for transfers between devices  379 us (39%)
  Pallas kernels  312 us (32%)
  blocking collectives  130 us (13%)
  local copies, waits for them, and re-layouts  46 us (5%)
  other arithmetic  43.2 us (4%)
  matrix products  21.2 us (2%)
  between operations  16.3 us (2%)
  starting transfers between devices  11.7 us (1%)
    reduce_scatter x4, waiting for transfers between devices, scatter_sum(): lax.psum_scatter(flat, 'tp', scatter_dimension=0, tiled=True)  251 us
    pallas_call x4, Pallas kernels, run_experts(): pl.pallas_call(functools.partial(expert_kernel, n_piece, has_acc, prev is...  205 us
    pallas_call x2, Pallas kernels, collect_rows(): pl.pallas_call(collect_kernel, grid_spec=pltpu.PrefetchScalarGridSpec(num...  71.9 us
    ppermute x11, waiting for transfers between devices, swap(): return lax.ppermute(v, 'ep', [(i, i ^ bit) for i in range(ep_size)])  56.8 us
    psum x1, blocking collectives, device_block(): stats = lax.psum(stats, 'ep')  55.1 us
    all_gather x2, waiting for transfers between devices, full(): return lax.all_gather(v, 'tp')  40.3 us
    pallas_call x3, Pallas kernels, widen_rows(): pl.pallas_call(widen_kernel, grid_spec=pltpu.PrefetchScalarGridSpec(num_s...  35.5 us
    all_gather x2, waiting for transfers between devices, device_block(): far.append(lax.all_gather(sent[c], 'tp', tiled=True))  24.6 us
  transfers between devices with their start and end apart: 20, of which 7 were waited for; matrix products, arithmetic and copies ran while one was open for 10% of the time, Pallas kernels for 32%

profile of v2, /device:TPU:0, one launch (start us, length us, event | category | flops | bytes accessed | tf_op | source)
XLA Modules:
  0.0 959.0 jit_solution(3896508283517970712)
XLA Ops:
  7.2 3.7 widen_rows.3
  11.0 3.2 collective-permute-start.2
  14.1 5.3 widen_rows.4
  19.4 26.5 %widen_rows.5.refs_0_ = bf16[8192,8,128]{2,1,0:T(8,128)(2,1)} custom-call(s32[1]{0:T(128)} %constant.197.clone.1.start_ref, bf16[8192,512]{1,0:T(8,128)(2,1)} %x_ref.4, bf16[8192,512]{1,0:T(8,128)(2,1)} %dy_ref.4), custom_call_target="tpu_custom_call" | custom-call | flops 8192000000 | bytes 33554432 | tf_op jit(solution)/shard_map/widen_rows/pallas_call | solution.py:38
  48.2 56.8 %collective-permute-done.4 = bf16[1280,8,128]{2,1,0:T(8,128)(2,1)} collective-permute-done((bf16[1280,8,128]{2,1,0:T(8,128)(2,1)}, bf16[1280,8,128]{2,1,0:T(8,128)(2,1)}, u32[]{:S(2)}, u32[]{:S(2)}) %collective-permute-start.4) | collective-permute-done | bytes 2621472 | tf_op jit(solution)/shard_map/ppermute | solution.py:307
  105.8 5.4 fusion.2
  111.3 2.9 fusion.85
  118.9 1.5 copy-done.11
  121.3 5.8 fusion
  128.0 6.0 fusion.29
  134.9 3.3 all-to-all-start
  138.3 4.8 all-to-all-done
  143.9 2.3 copy.145.refs_1_
  146.8 2.3 copy.144.refs_1_
  149.1 50.4 %experts_new.1 = (bf16[4,10240,128]{2,1,0:T(8,128)(2,1)}, bf16[4,10240,128]{2,1,0:T(8,128)(2,1)}, f32[8,512,512]{2,1,0:T(8,128)}, f32[8,512,512]{2,1,0:T(8,128)}, f32[8,512,512]{2,1,0:T(8,128)}) custom-call(s32[5120]{0:T(1024)} %max.29.idx_ref, bf16[8192,8,128]{2,1,0:T(8,128)(2,1)} %widen_rows.5.refs_0_, f32[8,640,2]{2,1,0:T(8,128)} %copy.144.refs_1_, ...), custom_call_target="tpu_custom_call" | custom-call | flops 24159191040 | bytes 65011712 | tf_op jit(solution)/shard_map/experts_new/pallas_call | solution.py:172
  199.5 51.3 %experts_acc.3 = (bf16[4,10240,128]{2,1,0:T(8,128)(2,1)}, bf16[4,10240,128]{2,1,0:T(8,128)(2,1)}, f32[8,512,512]{2,1,0:T(8,128)}, f32[8,512,512]{2,1,0:T(8,128)}, f32[8,512,512]{2,1,0:T(8,128)}) custom-call(s32[5120]{0:T(1024)} %max.27.idx_ref, ...), custom_call_target="tpu_custom_call", output_to_operand_aliasing={{2}: (7, {}), {3}: (8, {}), {4}: (9, {}), {0}: (10, {}), {1... | custom-call | flops 24159191040 | bytes 90177536 | tf_op jit(solution)/shard_map/experts_acc/pallas_call | solution.py:172
  251.3 24.5 %all-gather.8.cloned.1.call-done.refs_0_ = bf16[3072,8,128]{2,1,0:T(8,128)(2,1)} async-done(((bf16[768,8,128]{2,1,0:T(8,128)(2,1)}), bf16[3072,8,128]{2,1,0:T(8,128)(2,1)}) %all-gather.8.cloned.1.call-update) | async-done | bytes 6291472 | tf_op jit(solution)/shard_map/all_gather | solution.py:332
  277.3 2.3 copy.149.refs_2_
  279.7 2.3 copy.148.refs_2_
  283.3 51.6 %experts_acc.4 = (bf16[4,10240,128]{2,1,0:T(8,128)(2,1)}, bf16[4,10240,128]{2,1,0:T(8,128)(2,1)}, f32[8,512,512]{2,1,0:T(8,128)}, f32[8,512,512]{2,1,0:T(8,128)}, f32[8,512,512]{2,1,0:T(8,128)}) custom-call(s32[5120]{0:T(1024)} %add_select_fusion.6.idx_ref, ...), custom_call_target="tpu_custom_call", output_to_operand_aliasing={{2}: (8, {}), {3}: (9, {}), {4}: (10, {})} | custom-call | flops 24159191040 | bytes 90177536 | tf_op jit(solution)/shard_map/experts_acc/pallas_call | solution.py:172
  334.9 51.6 %experts_acc.5 = (bf16[4,10240,128]{2,1,0:T(8,128)(2,1)}, bf16[4,10240,128]{2,1,0:T(8,128)(2,1)}, f32[8,512,512]{2,1,0:T(8,128)}, f32[8,512,512]{2,1,0:T(8,128)}, f32[8,512,512]{2,1,0:T(8,128)}) custom-call(s32[5120]{0:T(1024)} %add_select_fusion.7.idx_ref, ...), custom_call_target="tpu_custom_call", output_to_operand_aliasing={{2}: (8, {}), {3}: (9, {}), {4}: (10, {}), {0}: (11, {}), {... | custom-call | flops 24159191040 | bytes 90177536 | tf_op jit(solution)/shard_map/experts_acc/pallas_call | solution.py:172
  388.0 2.9 fusion.83
  391.1 95.8 %reduce-scatter.7.cloned.1.call-done = bf16[10240,128]{1,0:T(8,128)(2,1)} async-done(((bf16[40960,128]{1,0:T(8,128)(2,1)}), bf16[10240,128]{1,0:T(8,128)(2,1)}) %reduce-scatter.7.cloned.1.call-update) | async-done | bytes 2621456 | tf_op jit(solution)/shard_map/reduce_scatter | solution.py:385
  486.9 3.4 fusion.82
  490.3 1.5 collective-permute-start.6
  492.5 97.1 %reduce-scatter.9.cloned.1.call-done = bf16[10240,128]{1,0:T(8,128)(2,1)} async-done(((bf16[40960,128]{1,0:T(8,128)(2,1)}), bf16[10240,128]{1,0:T(8,128)(2,1)}) %reduce-scatter.9.cloned.1.call-update) | async-done | bytes 2621456 | tf_op jit(solution)/shard_map/reduce_scatter | solution.py:385
  589.6 35.8 %collect_rows.2 = (f32[8192,128]{1,0:T(8,128)}, f32[8192,128]{1,0:T(8,128)}) custom-call(s32[2,8192]{1,0:T(2,128)S(1)} %pad_add_fusion.1.idx_ref, bf16[5120,128]{1,0:T(8,128)(2,1)S(1)} %get-tuple-element.100.refs_0_, bf16[5120,128]{1,0:T(8,128)(2,1)S(1)} %collective-permute-done.1.refs_1_, bf16[5120,128]{1,0:T(8,128)(2,1)} %collective-permute-done.6.refs_2_, ...), custom_call_target="tpu_custom_call" | custom-call | flops 20000000000 | bytes 14000000 | tf_op jit(solution)/shard_map/collect_rows/pallas_call | solution.py:235
  625.5 8.6 fusion.23
  634.1 58.2 %reduce-scatter.11.cloned.1.call-done = bf16[10240,128]{1,0:T(8,128)(2,1)} async-done(((bf16[40960,128]{1,0:T(8,128)(2,1)}), bf16[10240,128]{1,0:T(8,128)(2,1)}) %reduce-scatter.11.cloned.1.call-update) | async-done | bytes 2621456 | tf_op jit(solution)/shard_map/reduce_scatter | solution.py:385
  692.3 3.5 fusion.80
  695.8 1.5 collective-permute-start.9
  697.3 3.2 fusion.81
  702.0 55.1 %psum.42 = f32[65]{0:T(128)S(1)} all-reduce(f32[65]{0:T(128)S(1)} %pad_maximum_fusion.5), channel_id=1, replica_groups=mesh['tp'=4,'ep'=4] {'ep'}, use_global_device_ids=true, to_apply=%region_15.16 | all-reduce | flops 65 | bytes 520 | tf_op jit(solution)/shard_map/psum | solution.py:378
  757.8 1.5 multiply_reduce_fusion
  759.3 17.0 %psum.43 = f32[8192]{0:T(1024)S(1)} all-reduce(f32[8192]{0:T(1024)S(1)} %get-tuple-element.74), channel_id=1, replica_groups=mesh['tp'=4,'ep'=4] {'tp'}, use_global_device_ids=true, to_apply=%region_21.22 | all-reduce | flops 8192 | bytes 65536 | tf_op jit(solution)/shard_map/psum | solution.py:419
  776.2 14.7 %psum.44 = f32[8192]{0:T(1024)S(1)} all-reduce(f32[8192]{0:T(1024)S(1)} %get-tuple-element.68), channel_id=1, replica_groups=mesh['tp'=4,'ep'=4] {'tp'}, use_global_device_ids=true, to_apply=%region_22.23 | all-reduce | flops 8192 | bytes 65536 | tf_op jit(solution)/shard_map/psum | solution.py:421
  791.1 2.1 fusion.68
  793.2 36.0 %collect_rows.3 = (f32[8192,128]{1,0:T(8,128)}, f32[8192,128]{1,0:T(8,128)}) custom-call(s32[2,8192]{1,0:T(2,128)S(1)} %pad_add_fusion.1.idx_ref, bf16[5120,128]{1,0:T(8,128)(2,1)S(1)} %get-tuple-element.96.refs_0_, bf16[5120,128]{1,0:T(8,128)(2,1)} %collective-permute-done.8.refs_1_, bf16[5120,128]{1,0:T(8,128)(2,1)S(1)} %collective-permute-done.9.refs_2_, ...), custom_call_target="tpu_custom_call" | custom-call | flops 20000000000 | bytes 14000000 | tf_op jit(solution)/shard_map/collect_rows/pallas_call | solution.py:235
  829.2 6.6 fusion.18
  835.9 15.6 %psum.45 = f32[8192]{0:T(1024)S(1)} all-reduce(f32[8192]{0:T(1024)S(1)} %get-tuple-element.73), channel_id=1, replica_groups=mesh['tp'=4,'ep'=4] {'tp'}, use_global_device_ids=true, to_apply=%region_24.25 | all-reduce | flops 8192 | bytes 65536 | tf_op jit(solution)/shard_map/psum | solution.py:436
  851.5 8.2 fusion.24
  862.1 3.8 fusion.25
  865.9 11.1 %all-reduce.1 = (f32[128]{0:T(128)S(1)}, f32[128,32]{0,1:T(8,128)S(1)}) all-reduce(f32[128]{0:T(128)S(1)} %get-tuple-element.72, f32[128,32]{0,1:T(8,128)S(1)} %fusion.25), channel_id=1, replica_groups=mesh['tp'=4,'ep'=4] {'ep'}, use_global_device_ids=true, to_apply=%region_26.27 | all-reduce | flops 4224 | bytes 33792 | tf_op jit(solution)/shard_map/psum | solution.py:448
  876.9 7.3 all-gather.2
  884.2 8.8 all_gather.31
  893.1 9.2 copy.167
  902.3 40.3 %all-gather.14.cloned.1.call-done = bf16[32768,128]{1,0:T(8,128)(2,1)} async-done(((bf16[8192,128]{1,0:T(8,128)(2,1)}), bf16[32768,128]{1,0:T(8,128)(2,1)}) %all-gather.14.cloned.1.call-update) | async-done | bytes 8388624 | tf_op jit(solution)/shard_map/all_gather | solution.py:440
  942.6 8.2 copy.166
  (142 shorter events, 22.0 us)
Async XLA Ops:
  7.2 104.1 %copy-start = (f32[512,32]{0,1:T(8,128)S(1)}, f32[512,32]{0,1:T(8,128)}, u32[]{:S(2)}) copy-start(f32[512,32]{0,1:T(8,128)} %param.12) | copy-start | bytes 196612
  7.2 244.1 %all-gather.10.cloned.1.call-start = ((), (), s32[]{:S(2)}) async-start(), calls=%async_computation.7 | async-start | bytes 13107200 | tf_op jit(solution)/shard_map/all_gather | solution.py:332
  11.0 110.3 %collective-permute-start.2 = (bf16[768,8,128]{2,1,0:T(8,128)(2,1)}, bf16[768,8,128]{2,1,0:T(8,128)(2,1)}, u32[]{:S(2)}, u32[]{:S(2)}) collective-permute-start(bf16[768,8,128]{2,1,0:T(8,128)(2,1)} %widen_rows.3), channel_id=1, source_target_pairs={{0,2},{1,3},{2,0},{3,1},{4,6},{5,7},{6,4},{7,5},{8,10},{9,11},{10,... | collective-permute-start | bytes 4718600 | tf_op jit(solution)/shard_map/ppermute | solution.py:307
  19.4 26.5 %copy-start.9 = (s32[8192,2]{0,1:T(2,128)S(1)}, s32[8192,2]{0,1:T(2,128)}, u32[]{:S(2)}) copy-start(s32[8192,2]{0,1:T(2,128)} %param.10) | copy-start | bytes 196612
  19.4 85.6 %collective-permute-start.4 = (bf16[1280,8,128]{2,1,0:T(8,128)(2,1)}, bf16[1280,8,128]{2,1,0:T(8,128)(2,1)}, u32[]{:S(2)}, u32[]{:S(2)}) collective-permute-start(bf16[1280,8,128]{2,1,0:T(8,128)(2,1)} %widen_rows.4), channel_id=1, source_target_pairs={{0,2},{1,3},{2,0},{3,1},{4,6},{5,7},{6,4},{7,5},{8,10},{9,11},{10,... | collective-permute-start | bytes 7864328 | tf_op jit(solution)/shard_map/ppermute | solution.py:307
  45.9 153.5 %collective-permute-start = (bf16[8192,8,128]{2,1,0:T(8,128)(2,1)}, bf16[8192,8,128]{2,1,0:T(8,128)(2,1)}, u32[]{:S(2)}, u32[]{:S(2)}) collective-permute-start(bf16[8192,8,128]{2,1,0:T(8,128)(2,1)} %widen_rows.5.refs_0_), channel_id=1, source_target_pairs={{0,1},{1,0},{2,3},{3,2},{4,5},{5,4},{6,7},{7,6},{8,9},{9,8},{10,11... | collective-permute-start | bytes 50331656 | tf_op jit(solution)/shard_map/ppermute | solution.py:307
  46.0 72.8 %copy-start.3 = (s32[8192,1]{0,1:T(1,128)}, s32[8192,1]{0,1:T(1,128)S(1)}, u32[]{:S(2)}) copy-start(s32[8192,1]{0,1:T(1,128)S(1)} %get-tuple-element.113) | copy-start | bytes 98308
  46.0 81.1 %copy-start.5 = (s32[8192,1]{0,1:T(1,128)}, s32[8192,1]{0,1:T(1,128)S(1)}, u32[]{:S(2)}) copy-start(s32[8192,1]{0,1:T(1,128)S(1)} %get-tuple-element.114) | copy-start | bytes 98308
  105.1 170.8 %all-gather.8.cloned.1.call-start = ((), (), s32[]{:S(2)}) async-start(), calls=%async_computation.6 | async-start | bytes 7864320 | tf_op jit(solution)/shard_map/all_gather | solution.py:332
  105.3 6.0 slice-start
  105.8 5.5 slice-start.1
  105.8 5.5 copy-start.12
  111.3 2.9 copy-start.7
  114.2 1.0 copy-start.1
  118.9 1.5 copy-start.11
  134.9 8.3 all-to-all-start
  138.3 249.7 %reduce-scatter.5.cloned.1.call-start = ((), (), s32[]{:S(2)}) async-start(), calls=%async_computation.5 | async-start | bytes 13107200 | tf_op jit(solution)/shard_map/reduce_scatter | solution.py:385
  250.8 236.1 %reduce-scatter.7.cloned.1.call-start = ((), (), s32[]{:S(2)}) async-start(), calls=%async_computation.8 | async-start | bytes 13107200 | tf_op jit(solution)/shard_map/reduce_scatter | solution.py:385
  251.3 83.6 %collective-permute-start.5 = (bf16[5120,8,128]{2,1,0:T(8,128)(2,1)}, bf16[5120,8,128]{2,1,0:T(8,128)(2,1)}, u32[]{:S(2)}, u32[]{:S(2)}) collective-permute-start(bf16[5120,8,128]{2,1,0:T(8,128)(2,1)} %all-gather.10.cloned.1.call-done.refs_1_), channel_id=1, source_target_pairs={{0,1},{1,0},{2,3},{3,2},{4,5},{5,4},{6,7},{7,6},{8,9},{9,8},{10,11... | collective-permute-start | bytes 31457288 | tf_op jit(solution)/shard_map/ppermute | solution.py:307
  275.9 59.0 %collective-permute-start.3 = (bf16[3072,8,128]{2,1,0:T(8,128)(2,1)}, bf16[3072,8,128]{2,1,0:T(8,128)(2,1)}, u32[]{:S(2)}, u32[]{:S(2)}) collective-permute-start(bf16[3072,8,128]{2,1,0:T(8,128)(2,1)} %all-gather.8.cloned.1.call-done.refs_0_), channel_id=1, source_target_pairs={{0,1},{1,0},{2,3},{3,2},{4,5},{5,4},{6,7},{7,6},{8,9},{9,8},{10,11... | collective-permute-start | bytes 18874376 | tf_op jit(solution)/shard_map/ppermute | solution.py:307
  386.5 203.1 %reduce-scatter.9.cloned.1.call-start = ((), (), s32[]{:S(2)}) async-start(), calls=%async_computation.9 | async-start | bytes 13107200 | tf_op jit(solution)/shard_map/reduce_scatter | solution.py:385
  387.1 305.1 %reduce-scatter.11.cloned.1.call-start = ((), (), s32[]{:S(2)}) async-start(), calls=%async_computation.10 | async-start | bytes 13107200 | tf_op jit(solution)/shard_map/reduce_scatter | solution.py:385
  387.7 505.3 %all-gather.12.cloned.1.call-start = ((), (), s32[]{:S(2)}) async-start(), calls=%async_computation.11 | async-start | bytes 10485760 | tf_op jit(solution)/shard_map/all_gather | solution.py:440
  390.9 198.7 %collective-permute-start.1 = (bf16[5120,128]{1,0:T(8,128)(2,1)}, bf16[5120,128]{1,0:T(8,128)(2,1)S(1)}, u32[]{:S(2)}, u32[]{:S(2)}) collective-permute-start(bf16[5120,128]{1,0:T(8,128)(2,1)} %get-tuple-element.99), channel_id=1, source_target_pairs={{0,1},{1,0},{2,3},{3,2},{4,5},{5,4},{6,7},{7,6},{8,9},{9,8},{10,11... | collective-permute-start | bytes 3932168 | tf_op jit(solution)/shard_map/ppermute | solution.py:307
  490.3 99.3 %collective-permute-start.6 = (bf16[5120,128]{1,0:T(8,128)(2,1)}, bf16[5120,128]{1,0:T(8,128)(2,1)}, u32[]{:S(2)}, u32[]{:S(2)}) collective-permute-start(bf16[5120,128]{1,0:T(8,128)(2,1)} %get-tuple-element.98), channel_id=1, source_target_pairs={{0,2},{1,3},{2,0},{3,1},{4,6},{5,7},{6,4},{7,5},{8,10},{9,11},{10,... | collective-permute-start | bytes 3932168 | tf_op jit(solution)/shard_map/ppermute | solution.py:307
  491.8 97.8 %collective-permute-start.7 = (bf16[5120,128]{1,0:T(8,128)(2,1)}, bf16[5120,128]{1,0:T(8,128)(2,1)}, u32[]{:S(2)}, u32[]{:S(2)}) collective-permute-start(bf16[5120,128]{1,0:T(8,128)(2,1)} %get-tuple-element.97), channel_id=1, source_target_pairs={{0,3},{1,2},{2,1},{3,0},{4,7},{5,6},{6,5},{7,4},{8,11},{9,10},{10,... | collective-permute-start | bytes 3932168 | tf_op jit(solution)/shard_map/ppermute | solution.py:307
  634.0 308.5 %all-gather.14.cloned.1.call-start = ((), (), s32[]{:S(2)}) async-start(), calls=%async_computation.12 | async-start | bytes 10485760 | tf_op jit(solution)/shard_map/all_gather | solution.py:440
  695.8 95.3 %copy-start.4 = (s32[8192,1]{0,1:T(1,128)S(1)}, s32[8192,1]{0,1:T(1,128)}, u32[]{:S(2)}) copy-start(s32[8192,1]{0,1:T(1,128)} %copy-done.3) | copy-start | bytes 98308
  695.8 95.3 %copy-start.6 = (s32[8192,1]{0,1:T(1,128)S(1)}, s32[8192,1]{0,1:T(1,128)}, u32[]{:S(2)}) copy-start(s32[8192,1]{0,1:T(1,128)} %copy-done.5) | copy-start | bytes 98308
  695.8 95.3 %copy-start.10 = (f32[8192]{0:T(1024)S(1)}, f32[8192]{0:T(1024)}, u32[]{:S(2)}) copy-start(f32[8192]{0:T(1024)} %get-tuple-element.86) | copy-start | bytes 98308
  695.8 97.4 %collective-permute-start.9 = (bf16[5120,128]{1,0:T(8,128)(2,1)}, bf16[5120,128]{1,0:T(8,128)(2,1)S(1)}, u32[]{:S(2)}, u32[]{:S(2)}) collective-permute-start(bf16[5120,128]{1,0:T(8,128)(2,1)} %get-tuple-element.94), channel_id=1, source_target_pairs={{0,2},{1,3},{2,0},{3,1},{4,6},{5,7},{6,4},{7,5},{8,10},{9,11},{10,... | collective-permute-start | bytes 3932168 | tf_op jit(solution)/shard_map/ppermute | solution.py:307
  697.3 95.9 %collective-permute-start.10 = (bf16[5120,128]{1,0:T(8,128)(2,1)}, bf16[5120,128]{1,0:T(8,128)(2,1)}, u32[]{:S(2)}, u32[]{:S(2)}) collective-permute-start(bf16[5120,128]{1,0:T(8,128)(2,1)} %get-tuple-element.93), channel_id=1, source_target_pairs={{0,3},{1,2},{2,1},{3,0},{4,7},{5,6},{6,5},{7,4},{8,11},{9,10},{10,... | collective-permute-start | bytes 3932168 | tf_op jit(solution)/shard_map/ppermute | solution.py:307
  700.5 92.7 %collective-permute-start.8 = (bf16[5120,128]{1,0:T(8,128)(2,1)}, bf16[5120,128]{1,0:T(8,128)(2,1)}, u32[]{:S(2)}, u32[]{:S(2)}) collective-permute-start(bf16[5120,128]{1,0:T(8,128)(2,1)} %get-tuple-element.95), channel_id=1, source_target_pairs={{0,1},{1,0},{2,3},{3,2},{4,5},{5,4},{6,7},{7,6},{8,9},{9,8},{10,11... | collective-permute-start | bytes 3932168 | tf_op jit(solution)/shard_map/ppermute | solution.py:307
  793.2 36.1 %copy-start.8 = (f32[8192]{0:T(1024)S(1)}, f32[8192]{0:T(1024)}, u32[]{:S(2)}) copy-start(f32[8192]{0:T(1024)} %copy-done.7) | copy-start | bytes 98308
  851.4 10.7 %copy-start.2 = (f32[8192,32]{0,1:T(8,128)S(1)}, f32[8192,32]{0,1:T(8,128)}, u32[]{:S(2)}) copy-start(f32[8192,32]{0,1:T(8,128)} %copy-done.1) | copy-start | bytes 3145732
Sparse Core Ops, SparseCore 0:
  105.2 102.5 all-gather.9
  209.6 66.2 all-gather.7
  278.9 99.7 reduce-scatter.4
  386.7 100.2 reduce-scatter.6
  489.9 99.7 reduce-scatter.8
  592.5 99.7 reduce-scatter.10
  694.1 85.0 all-gather.11
  859.8 82.7 all-gather.13
